TPU v7x, 64 devices: a 2x2x8 block of a 4x4x8 slice. The times are simulated.
64 devices in a mesh: rep: 8 (over x, y, core), dp: 8 (over z).
Axes of the slice: x: 2, y: 2, z: 8, core: 2. Of those that a mesh axis runs over, the one named last changes fastest.
The devices are a block of a 4x4x8 slice.
Arguments:
- x: bfloat16 [64, 2048, 640], P(('rep', 'dp')), parts along dimension 0
- dy: bfloat16 [64, 2048, 640], P(('rep', 'dp')), parts along dimension 0
- w_gate: bfloat16 [2, 640, 1792], replicated
- w_up: bfloat16 [2, 640, 1792], replicated
- w_down: bfloat16 [2, 1792, 640], replicated
- m_w_gate: float32 [2, 640, 1792], replicated
- m_w_up: float32 [2, 640, 1792], replicated
- m_w_down: float32 [2, 1792, 640], replicated
- v_w_gate: float32 [2, 640, 1792], replicated
- v_w_up: float32 [2, 640, 1792], replicated
- v_w_down: float32 [2, 1792, 640], replicated
Outputs:
- output 1: bfloat16 [16, 640, 1792], P('rep'), parts along dimension 0
- output 2: bfloat16 [16, 640, 1792], P('rep'), parts along dimension 0
- output 3: bfloat16 [16, 1792, 640], P('rep'), parts along dimension 0
- output 4: float32 [16, 640, 1792], P('rep'), parts along dimension 0
- output 5: float32 [16, 640, 1792], P('rep'), parts along dimension 0
- output 6: float32 [16, 1792, 640], P('rep'), parts along dimension 0
- output 7: float32 [16, 640, 1792], P('rep'), parts along dimension 0
- output 8: float32 [16, 640, 1792], P('rep'), parts along dimension 0
- output 9: float32 [16, 1792, 640], P('rep'), parts along dimension 0
There are 8 independent parts. A program takes and returns all parts, laid end to end along the dimension named above; an argument that names none is the same for every part.
All inputs are finite; a program needn't handle non-finite values.
Results may differ from a plain program's by a relative error of at most 0.02.
Values are sent between devices in bfloat16 or wider.
A program may use at most 768 MiB of HBM per device.

v0:
```python
import jax
import jax.numpy as jnp
from jax import lax
from jax.sharding import PartitionSpec as P

NAMES = ("w_gate", "w_up", "w_down")


def matmul(a, w):
    return jnp.dot(a, w, preferred_element_type=jnp.float32).astype(jnp.bfloat16)


def normed(h):
    wide = h.astype(jnp.float32)
    scale = lax.rsqrt(jnp.mean(wide**2, -1, keepdims=True) + 1e-6)
    return (wide * scale).astype(jnp.bfloat16)


def layer(h, w):
    a = normed(h)
    gate = jnp.dot(a, w["w_gate"], preferred_element_type=jnp.float32)
    up = jnp.dot(a, w["w_up"], preferred_element_type=jnp.float32)
    return h + matmul((jax.nn.silu(gate) * up).astype(jnp.bfloat16), w["w_down"])


def adamw(w, m, v, g):
    m = 0.9 * m + 0.1 * g
    v = 0.95 * v + 0.05 * g * g
    step = m * lax.rsqrt(v + 1e-8) + 0.1 * w
    return (w - 0.02 * step).astype(jnp.bfloat16), m, v


def solution(mesh):
    def step(x, dy, *arrays):
        weights, m, v = (arrays[i : i + 3] for i in (0, 3, 6))
        layers = weights[0].shape[0]
        h, kept = x[0], []
        for number in range(layers):
            kept.append(h)
            h = layer(h, {name: w[number] for name, w in zip(NAMES, weights, strict=True)})
        by_h, summed = dy[0], [None] * layers
        for number in reversed(range(layers)):
            _, back = jax.vjp(lambda w, h: layer(h, w), {name: w[number] for name, w in zip(NAMES, weights, strict=True)}, kept[number])
            by_w, by_h = back(by_h)
            summed[number] = [lax.psum(by_w[name], "dp") for name in NAMES]
        gradients = [jnp.stack([summed[number][i] for number in range(layers)]).astype(jnp.float32) for i in range(3)]
        new = [adamw(w.astype(jnp.float32), m, v, g) for w, m, v, g in zip(weights, m, v, gradients, strict=True)]
        return tuple(one[which] for which in range(3) for one in new)

    return jax.shard_map(
        step,
        mesh=mesh,
        in_specs=(P(("rep", "dp"), None, None),) * 2 + (P(None, None, None),) * 9,
        out_specs=(P("rep", None, None),) * 9,
        check_vma=False,
    )
```

profile of v0, /device:TPU:21, one launch (start us, length us, event | category | flops | bytes accessed | tf_op | source)
XLA Modules:
  0.0 541.8 jit_solution(10682438142334474603)
XLA Ops:
  7.2 0.1 all-reduce.3.cloned.1.call-start
  7.3 3.0 copy.20
  10.3 0.0 copy-start.1
  10.3 0.6 fusion.30
  10.8 4.7 copy.21
  15.6 10.1 %convolution_convert_fusion.1 = bf16[2048,1792]{1,0:T(8,128)(2,1)} fusion(bf16[1,2048,640]{2,1,0:T(8,128)(2,1)} %param.12, bf16[2,1792,640]{2,1,0:T(8,128)(2,1)} %param.15), kind=kOutput, calls=%fused_computation.54 | convolution fusion | flops 4701290496 | bytes 12255232 | tf_op jit(solution)/shard_map/transpose(jvp())/dot_general | solution.py:10
  25.7 11.0 %fusion.71 = f32[2048,1792]{1,0:T(8,128)} fusion(bf16[2,640,1792]{2,1,0:T(8,128)(2,1)} %param.13, bf16[1,2048,640]{2,1,0:T(8,128)(2,1)S(1)} %copy-done.5, f32[2048]{0:T(1024)S(1)} %add_rsqrt_fusion), kind=kOutput, calls=%fused_computation.103 | convolution fusion | flops 4701552640 | bytes 19603456 | tf_op jit(solution)/shard_map/dot_general | solution.py:21
  36.7 0.0 copy-done.9
  36.7 17.1 %multiply_convert_fusion.1 = (bf16[2048,1792]{1,0:T(8,128)(2,1)}, f32[2048,1792]{1,0:T(8,128)}) fusion(f32[2048,1792]{1,0:T(8,128)} %fusion.71, bf16[2,640,1792]{2,1,0:T(8,128)(2,1)} %param.14, bf16[1,2048,640]{2,1,0:T(8,128)(2,1)S(1)} %copy-done.5, f32[2048]{0:T(1024)S(1)} %add_rsqrt_fusion), kind=kOutput, calls=%fused_computation.17 | convolution fusion | flops 4723572736 | bytes 41623552 | tf_op jit(solution)/shard_map/dot_general | solution.py:22
  53.8 0.0 copy-done.1
  53.8 0.0 slice-done
  53.8 0.0 slice-done.1
  53.8 8.5 %fusion.34 = (f32[2048]{0:T(1024)S(1)}, bf16[2048,640]{0,1:T(8,128)(2,1)S(1)}) fusion(bf16[2048,1792]{1,0:T(8,128)(2,1)} %get-tuple-element.24, bf16[2,1792,640]{2,1,0:T(8,128)(2,1)S(1)} %bitcast.71, bf16[1,2048,640]{1,2,0:T(8,128)(2,1)S(1)} %copy.20), kind=kOutput, calls=%fused_computation.64 | convolution fusion | flops 4704172032 | bytes 14884864 | tf_op jit(solution)/shard_map/dot_general | solution.py:10
  62.3 0.0 copy-start.3
  62.3 0.0 copy-start.7
  62.4 1.5 copy-done.3
  63.8 10.8 %fusion.60 = f32[2048,1792]{1,0:T(8,128)} fusion(bf16[2,640,1792]{2,1,0:T(8,128)(2,1)} %param.14, bf16[2048,640]{0,1:T(8,128)(2,1)S(1)} %get-tuple-element.27, f32[2048]{0:T(1024)S(1)} %fusion.88), kind=kOutput, calls=%fused_computation.92 | convolution fusion | flops 4701552640 | bytes 19603456 | tf_op jit(solution)/shard_map/jvp()/dot_general | solution.py:22
  74.6 23.2 %fusion.2 = (bf16[2048,1792]{1,0:T(8,128)(2,1)}, f32[2048,1792]{1,0:T(8,128)}) fusion(f32[2048,1792]{1,0:T(8,128)} %fusion.60, bf16[2048,1792]{1,0:T(8,128)(2,1)} %convolution_convert_fusion.1, bf16[2,640,1792]{2,1,0:T(8,128)(2,1)} %param.13, bf16[2048,640]{0,1:T(8,128)(2,1)} %copy-done.3, f32[2048]{0:T(1024)S(1)} %fusion.88), kind=kOutput, calls=%fused_computation.8 | convolution fusion | flops 4745592832 | bytes 48963584 | tf_op jit(solution)/shard_map/jvp()/dot_general | solution.py:21
  97.9 0.0 slice-start.9
  97.9 13.9 %fusion.51 = bf16[1,1792,640]{2,1,0:T(8,128)(2,1)} fusion(f32[2048,1792]{1,0:T(8,128)} %fusion.60, bf16[1,2048,640]{2,1,0:T(8,128)(2,1)S(1)} %copy-done.6, f32[2048,1792]{1,0:T(8,128)} %get-tuple-element.29), kind=kOutput, calls=%fused_computation.85 | convolution fusion | flops 4720787456 | bytes 34275328 | tf_op jit(solution)/shard_map/transpose(jvp())/dot_general | solution.py:10
  111.8 11.8 %fusion.50 = bf16[1,640,1792]{2,1,0:T(8,128)(2,1)} fusion(bf16[2048,1792]{1,0:T(8,128)(2,1)} %convolution_convert_fusion.1, bf16[2048,640]{0,1:T(8,128)(2,1)S(1)} %copy-done.4, f32[2048]{0:T(1024)S(1)} %fusion.88, f32[2048,1792]{1,0:T(8,128)} %get-tuple-element.29), kind=kOutput, calls=%fused_computation.84 | convolution fusion | flops 4724719616 | bytes 26943488 | tf_op jit(solution)/shard_map/transpose(jvp())/dot_general | solution.py:22
  123.6 0.0 slice-done.9
  123.6 0.0 slice-start.5
  123.6 10.1 %fusion.38 = bf16[2048,640]{0,1:T(8,128)(2,1)S(1)} fusion(bf16[2048,1792]{1,0:T(8,128)(2,1)} %convolution_convert_fusion.1, bf16[2,640,1792]{2,1,0:T(8,128)(2,1)S(1)} %bitcast.79, f32[2048,1792]{1,0:T(8,128)} %get-tuple-element.29), kind=kOutput, calls=%fused_computation.72 | convolution fusion | flops 4720951296 | bytes 26935296 | tf_op jit(solution)/shard_map/transpose(jvp())/dot_general | solution.py:22
  133.7 0.0 slice-start.10
  133.7 0.0 slice-start.11
  133.7 9.4 %fusion.47 = bf16[1,640,1792]{2,1,0:T(8,128)(2,1)} fusion(bf16[2048,1792]{1,0:T(8,128)(2,1)} %get-tuple-element.28, bf16[2048,640]{0,1:T(8,128)(2,1)S(1)} %copy-done.4, f32[2048]{0:T(1024)S(1)} %fusion.88), kind=kOutput, calls=%fused_computation.81 | convolution fusion | flops 4701552640 | bytes 12263424 | tf_op jit(solution)/shard_map/transpose(jvp())/dot_general | solution.py:21
  143.1 0.0 slice-done.5
  143.1 0.0 copy-start
  143.1 8.8 %fusion.36 = (f32[2048]{0:T(1024)S(1)}, bf16[2048,640]{0,1:T(8,128)(2,1)S(1)}) fusion(bf16[2048,640]{0,1:T(8,128)(2,1)S(1)} %copy-done.4, bf16[2048,640]{0,1:T(8,128)(2,1)S(1)} %fusion.38, bf16[2048,1792]{1,0:T(8,128)(2,1)} %get-tuple-element.28, bf16[2,640,1792]{2,1,0:T(8,128)(2,1)S(1)} %bitcast.75), kind=kOutput, calls=%fused_computation.66 | convolution fusion | flops 4704172032 | bytes 17506304 | tf_op jit(solution)/shard_map/transpose(jvp())/dot_general | solution.py:21
  151.9 0.0 slice-start.2
  151.9 1.8 fusion.53
  153.7 0.0 slice-done.10
  153.8 0.0 slice-done.11
  153.8 0.0 slice-start.3
  153.8 7.4 %fusion.48 = bf16[1,1792,640]{2,1,0:T(8,128)(2,1)} fusion(bf16[2048,1792]{1,0:T(8,128)(2,1)S(1)} %bitcast.81, bf16[2048,640]{0,1:T(8,128)(2,1)S(1)} %fusion.53), kind=kOutput, calls=%fused_computation.82 | convolution fusion | flops 4698767360 | bytes 12255232 | tf_op jit(solution)/shard_map/transpose(jvp())/dot_general | solution.py:10
  161.2 0.0 slice-done.3
  161.2 0.0 copy-start.10
  161.2 6.2 %convolution_convert_fusion = bf16[2048,1792]{1,0:T(8,128)(2,1)S(1)} fusion(bf16[2048,640]{0,1:T(8,128)(2,1)S(1)} %fusion.53, bf16[2,1792,640]{2,1,0:T(8,128)(2,1)S(1)} %bitcast.73), kind=kOutput, calls=%fused_computation.53 | convolution fusion | flops 4701290496 | bytes 12255232 | tf_op jit(solution)/shard_map/transpose(jvp())/dot_general | solution.py:10
  167.4 0.0 copy-done.2
  167.4 0.0 copy-done.10
  167.4 0.0 copy-start.11
  167.4 13.2 %fusion.49 = bf16[1,640,1792]{2,1,0:T(8,128)(2,1)} fusion(bf16[2048,1792]{1,0:T(8,128)(2,1)S(1)} %convolution_convert_fusion, f32[2048,1792]{1,0:T(8,128)} %fusion.71, bf16[1,2048,640]{1,2,0:T(8,128)(2,1)S(1)} %copy-done.2, f32[2048]{0:T(1024)S(1)} %copy-done.10), kind=kOutput, calls=%fused_computation.83 | convolution fusion | flops 4724719616 | bytes 26943488 | tf_op jit(solution)/shard_map/transpose(jvp())/dot_general | solution.py:22
  180.6 17.1 %fusion.44 = bf16[1,640,1792]{2,1,0:T(8,128)(2,1)} fusion(f32[2048,1792]{1,0:T(8,128)} %fusion.71, f32[2048,1792]{1,0:T(8,128)} %get-tuple-element.25, bf16[2048,1792]{1,0:T(8,128)(2,1)} %copy-done.11, bf16[1,2048,640]{1,2,0:T(8,128)(2,1)S(1)} %copy-done.2, f32[2048]{0:T(1024)S(1)} %copy-done.10), kind=kOutput, calls=%fused_computation.80 | convolution fusion | flops 4743069696 | bytes 41623552 | tf_op jit(solution)/shard_map/transpose(jvp())/dot_general | solution.py:21
  197.7 0.1 all-reduce.3.cloned.1.call-update
  197.8 287.2 %all-reduce.3.cloned.1.call-done = (bf16[1,640,1792]{2,1,0:T(8,128)(2,1)}, bf16[1,640,1792]{2,1,0:T(8,128)(2,1)}, bf16[1,640,1792]{2,1,0:T(8,128)(2,1)}, bf16[1,...) async-done(((bf16[1,640,1792]{2,1,0:T(8,128)(2,1)}, bf16[1,640,1792]{2,1,0:T(8,128)(2,1)}, bf16[1,640,1792]{2,1,0:T(8,128)(2,1)}, ...) | async-done | bytes 13762576 | tf_op jit(solution)/shard_map/psum | solution.py:45
  485.0 19.5 %fusion.23 = (bf16[2,1792,640]{2,1,0:T(8,128)(2,1)}, f32[2,1792,640]{2,1,0:T(8,128)}, f32[2,1792,640]{2,1,0:T(8,128)}) fusion(bf16[2,1792,640]{2,1,0:T(8,128)(2,1)} %param.15, bf16[1,1792,640]{2,1,0:T(8,128)(2,1)} %get-tuple-element.13, bf16[1,1792,640]{2,1,0:T(8,128)(2,1)} %get-tuple-element.14, f32[2,1792,640]{2,1,0:T(8,128)} %param.21, ...), kind=kLoop, calls=%fused_computation.44 | loop fusion | flops 43581440 | bytes 50462720 | tf_op jit(solution)/shard_map/convert_element_type | solution.py:30
  504.4 30.0 %fusion.15 = (bf16[2,640,1792]{2,1,0:T(8,128)(2,1)}, f32[2,640,1792]{2,1,0:T(8,128)}, f32[2,640,1792]{2,1,0:T(8,128)}, bf16[2,640,1792]{2,1,0:T(8,128)(2,1)}, f3...) fusion(bf16[2,640,1792]{2,1,0:T(8,128)(2,1)S(1)} %bitcast.77, bf16[1,640,1792]{2,1,0:T(8,128)(2,1)} %get-tuple-element.9, ...), kind=kLoop, calls=%fused_computation.36 | loop fusion | flops 87162880 | bytes 100925440 | tf_op jit(solution)/shard_map/convert_element_type | solution.py:30
  (33 shorter events, 0.1 us)
Async XLA Ops:
  7.2 477.8 %all-reduce.3.cloned.1.call-start = ((), (), s32[]{:S(2)}) async-start(), calls=%async_computation | async-start | bytes 27525120 | tf_op jit(solution)/shard_map/psum | solution.py:45
  10.3 43.5 %copy-start.1 = (bf16[1,2048,640]{1,2,0:T(8,128)(2,1)}, bf16[1,2048,640]{1,2,0:T(8,128)(2,1)S(1)}, u32[]{:S(2)}) copy-start(bf16[1,2048,640]{1,2,0:T(8,128)(2,1)S(1)} %copy.20) | copy-start | bytes 7864324
  10.8 25.8 %copy-start.9 = (f32[2048]{0:T(1024)}, f32[2048]{0:T(1024)S(1)}, u32[]{:S(2)}) copy-start(f32[2048]{0:T(1024)S(1)} %add_rsqrt_fusion) | copy-start | bytes 24580
  15.6 10.1 %copy-start.5 = (bf16[1,2048,640]{2,1,0:T(8,128)(2,1)S(1)}, bf16[1,2048,640]{2,1,0:T(8,128)(2,1)}, u32[]{:S(2)}) copy-start(bf16[1,2048,640]{2,1,0:T(8,128)(2,1)} %param.11) | copy-start | bytes 7864324
  25.7 28.1 %slice-start = ((s8[4587520]{0:T(1024)(128)(4,1)}), s8[4194304]{0:T(1024)(128)(4,1)S(1)}, s32[]{:S(2)}) async-start(s8[4587520]{0:T(1024)(128)(4,1)} %bitcast.70), calls=%async_computation.1 | async-start | bytes 8388608
  36.7 17.1 %slice-start.1 = ((s8[4587520]{0:T(1024)(128)(4,1)}), s8[393216]{0:T(1024)(128)(4,1)S(1)}, s32[]{:S(2)}) async-start(s8[4587520]{0:T(1024)(128)(4,1)} %bitcast.70), calls=%async_computation.2 | async-start | bytes 786432
  62.3 1.5 copy-start.3
  62.3 1.5 copy-start.7
  74.6 23.3 %copy-start.6 = (bf16[1,2048,640]{2,1,0:T(8,128)(2,1)S(1)}, bf16[1,2048,640]{2,1,0:T(8,128)(2,1)}, u32[]{:S(2)}) copy-start(bf16[1,2048,640]{2,1,0:T(8,128)(2,1)} %param.12) | copy-start | bytes 7864324
  74.6 49.0 %slice-start.8 = ((s8[4587520]{0:T(1024)(128)(4,1)}), s8[393216]{0:T(1024)(128)(4,1)S(1)}, s32[]{:S(2)}) async-start(s8[4587520]{0:T(1024)(128)(4,1)} %bitcast.78), calls=%async_computation.9 | async-start | bytes 786432
  97.8 13.9 %copy-start.4 = (bf16[2048,640]{0,1:T(8,128)(2,1)S(1)}, bf16[2048,640]{0,1:T(8,128)(2,1)}, u32[]{:S(2)}) copy-start(bf16[2048,640]{0,1:T(8,128)(2,1)} %copy-done.3) | copy-start | bytes 7864324
  97.9 25.7 %slice-start.9 = ((s8[4587520]{0:T(1024)(128)(4,1)}), s8[4194304]{0:T(1024)(128)(4,1)S(1)}, s32[]{:S(2)}) async-start(s8[4587520]{0:T(1024)(128)(4,1)} %bitcast.78), calls=%async_computation.10 | async-start | bytes 8388608
  111.8 31.3 %slice-start.4 = ((s8[4587520]{0:T(1024)(128)(4,1)}), s8[4194304]{0:T(1024)(128)(4,1)S(1)}, s32[]{:S(2)}) async-start(s8[4587520]{0:T(1024)(128)(4,1)} %bitcast.74), calls=%async_computation.5 | async-start | bytes 8388608
  123.6 19.5 %slice-start.5 = ((s8[4587520]{0:T(1024)(128)(4,1)}), s8[393216]{0:T(1024)(128)(4,1)S(1)}, s32[]{:S(2)}) async-start(s8[4587520]{0:T(1024)(128)(4,1)} %bitcast.74), calls=%async_computation.6 | async-start | bytes 786432
  133.7 20.1 %slice-start.10 = ((s8[7340032]{0:T(1024)(128)(4,1)}), s8[4194304]{0:T(1024)(128)(4,1)S(1)}, s32[]{:S(2)}) async-start(s8[7340032]{0:T(1024)(128)(4,1)} %bitcast.80), calls=%async_computation.11 | async-start | bytes 8388608
  133.7 20.1 %slice-start.11 = ((s8[7340032]{0:T(1024)(128)(4,1)}), s8[3145728]{0:T(1024)(128)(4,1)S(1)}, s32[]{:S(2)}) async-start(s8[7340032]{0:T(1024)(128)(4,1)} %bitcast.80), calls=%async_computation.12 | async-start | bytes 6291456
  143.1 8.8 %copy-start.8 = (f32[2048]{0:T(1024)S(1)}, f32[2048]{0:T(1024)}, u32[]{:S(2)}) copy-start(f32[2048]{0:T(1024)} %copy-done.7) | copy-start | bytes 24580
  143.1 8.8 %copy-start = (bf16[1,2048,640]{1,2,0:T(8,128)(2,1)S(1)}, bf16[1,2048,640]{1,2,0:T(8,128)(2,1)}, u32[]{:S(2)}) copy-start(bf16[1,2048,640]{1,2,0:T(8,128)(2,1)} %copy.21) | copy-start | bytes 7864324
  151.9 9.3 %slice-start.2 = ((s8[4587520]{0:T(1024)(128)(4,1)}), s8[393216]{0:T(1024)(128)(4,1)S(1)}, s32[]{:S(2)}) async-start(s8[4587520]{0:T(1024)(128)(4,1)} %bitcast.72), calls=%async_computation.3 | async-start | bytes 786432
  153.8 7.4 %slice-start.3 = ((s8[4587520]{0:T(1024)(128)(4,1)}), s8[4194304]{0:T(1024)(128)(4,1)S(1)}, s32[]{:S(2)}) async-start(s8[4587520]{0:T(1024)(128)(4,1)} %bitcast.72), calls=%async_computation.4 | async-start | bytes 8388608
  161.2 6.2 %copy-start.2 = (bf16[1,2048,640]{1,2,0:T(8,128)(2,1)S(1)}, bf16[1,2048,640]{1,2,0:T(8,128)(2,1)}, u32[]{:S(2)}) copy-start(bf16[1,2048,640]{1,2,0:T(8,128)(2,1)} %copy-done.1) | copy-start | bytes 7864324
  161.2 6.2 %copy-start.10 = (f32[2048]{0:T(1024)S(1)}, f32[2048]{0:T(1024)}, u32[]{:S(2)}) copy-start(f32[2048]{0:T(1024)} %copy-done.9) | copy-start | bytes 24580
  167.4 13.2 %copy-start.11 = (bf16[2048,1792]{1,0:T(8,128)(2,1)}, bf16[2048,1792]{1,0:T(8,128)(2,1)S(1)}, u32[]{:S(2)}) copy-start(bf16[2048,1792]{1,0:T(8,128)(2,1)S(1)} %convolution_convert_fusion) | copy-start | bytes 22020100
  197.7 306.7 %slice-start.6 = ((s8[4587520]{0:T(1024)(128)(4,1)}), s8[393216]{0:T(1024)(128)(4,1)S(1)}, s32[]{:S(2)}) async-start(s8[4587520]{0:T(1024)(128)(4,1)} %bitcast.76), calls=%async_computation.7 | async-start | bytes 786432
  485.0 19.5 %slice-start.7 = ((s8[4587520]{0:T(1024)(128)(4,1)}), s8[4194304]{0:T(1024)(128)(4,1)S(1)}, s32[]{:S(2)}) async-start(s8[4587520]{0:T(1024)(128)(4,1)} %bitcast.76), calls=%async_computation.8 | async-start | bytes 8388608
Sparse Core Ops, SparseCore 0:
  197.9 287.0 all-reduce.2
where the time goes:
time: 548 us; the launch traced here: 542 us
  waiting for transfers between devices  287 us (52%)
  matrix products  179 us (33%)
  other arithmetic  51.8 us (9%)
  between operations  14.8 us (3%)
  local copies, waits for them, and re-layouts  9.28 us (2%)
    psum x1, waiting for transfers between devices, step(): summed[number] = [lax.psum(by_w[name], 'dp') for name in NAMES]  287 us
    dot_general x5, matrix products, layer(): gate = jnp.dot(a, w['w_gate'], preferred_element_type=jnp.float32)  69.5 us
    dot_general x5, matrix products, layer(): up = jnp.dot(a, w['w_up'], preferred_element_type=jnp.float32)  62.9 us
    convert_element_type x2, other arithmetic, adamw(): return ((w - 0.02 * step).astype(jnp.bfloat16), m, v)  49.5 us
    dot_general x5, matrix products, matmul(): jnp.dot(a, w, preferred_element_type=jnp.float32).astype(jnp.bfloat16)  46.1 us
  transfers between devices with their start and end apart: 1, of which 1 were waited for; matrix products, arithmetic and copies ran while one was open for 0% of the time, Pallas kernels for 0%

commit v1 on v0

v1 whole, which is shorter than its diff:
```python
import functools

import jax
import jax.numpy as jnp
from jax import lax
from jax.experimental import pallas as pl
from jax.experimental.pallas import tpu as pltpu
from jax.sharding import PartitionSpec as P


F32, BF16 = jnp.float32, jnp.bfloat16
COLS = 256
ROWS = 1024
VMEM_LIMIT = 60 * 1024 * 1024


def dot(a, b, contract):
    return lax.dot_general(a, b, ((contract[:1], contract[1:]), ((), ())), preferred_element_type=F32)


def params(*semantics):
    return pltpu.CompilerParams(dimension_semantics=semantics, vmem_limit_bytes=VMEM_LIMIT)


def cost(flops, *arrays):
    return pl.CostEstimate(flops=flops, bytes_accessed=sum(a.size * a.dtype.itemsize for a in arrays), transcendentals=0)


def shaped(shape, dtype=BF16):
    return jax.ShapeDtypeStruct(shape, dtype)


def norm_scale(wide):
    return lax.rsqrt(jnp.mean(wide * wide, -1, keepdims=True) + 1e-6)


def forward_kernel(h_ref, wg_ref, wu_ref, wd_ref, next_ref, a_ref, act_ref, acc_ref):
    j = pl.program_id(1)

    @pl.when(j == 0)
    def _():
        wide = h_ref[...].astype(F32)
        a_ref[...] = (wide * norm_scale(wide)).astype(BF16)
        acc_ref[...] = jnp.zeros_like(acc_ref)

    a = a_ref[...]
    gate = dot(a, wg_ref[...], (1, 0))
    up = dot(a, wu_ref[...], (1, 0))
    act = (gate * jax.nn.sigmoid(gate) * up).astype(BF16)
    act_ref[...] = act
    acc_ref[...] += dot(act, wd_ref[...], (1, 0))

    @pl.when(j == pl.num_programs(1) - 1)
    def _():
        down = acc_ref[...].astype(BF16).astype(F32)
        next_ref[...] = (h_ref[...].astype(F32) + down).astype(BF16)


def forward(h, wg, wu, wd, number):
    tokens, d = h.shape
    ff = wg.shape[2]
    rows = min(tokens, ROWS)
    by_rows = pl.BlockSpec((rows, d), lambda i, j: (i, 0))
    into = pl.BlockSpec((None, d, COLS), lambda i, j: (number, 0, j))
    out_of = pl.BlockSpec((None, COLS, d), lambda i, j: (number, j, 0))
    return pl.pallas_call(
        forward_kernel,
        grid=(tokens // rows, ff // COLS),
        in_specs=[by_rows, into, into, out_of],
        out_specs=[by_rows, by_rows, pl.BlockSpec((rows, COLS), lambda i, j: (i, j))],
        out_shape=[shaped((tokens, d)), shaped((tokens, d)), shaped((tokens, ff))],
        scratch_shapes=[pltpu.VMEM((rows, d), F32)],
        compiler_params=params("parallel", "arbitrary"),
        cost_estimate=cost(6 * tokens * d * ff, h, h, h),
    )(h, wg, wu, wd)


def gate_kernel(n_outs, h_ref, dy_ref, wg_ref, wu_ref, wd_ref, *refs):
    dg_ref, du_ref, a_ref, *act_ref = refs[-n_outs:]
    j = pl.program_id(1)

    @pl.when(j == 0)
    def _():
        wide = h_ref[...].astype(F32)
        a_ref[...] = (wide * norm_scale(wide)).astype(BF16)

    a = a_ref[...]
    gate = dot(a, wg_ref[...], (1, 0))
    up = dot(a, wu_ref[...], (1, 0))
    by_act = dot(dy_ref[...], wd_ref[...], (1, 1)).astype(BF16).astype(F32)
    s = jax.nn.sigmoid(gate)
    silu = gate * s
    if act_ref:
        act_ref[0][...] = (silu * up).astype(BF16)
    du_ref[...] = (by_act * silu).astype(BF16)
    dg_ref[...] = (by_act * up * (s + silu * (1.0 - s))).astype(BF16)


def gate_backward(h, dy, wg, wu, wd, number, with_act, part=0, parts=1, so_far=None):
    tokens, d = h.shape
    ff = wg.shape[2]
    rows = min(tokens // parts, ROWS)
    tiles = tokens // rows // parts
    first = part * tiles
    by_rows = pl.BlockSpec((rows, d), lambda i, j: (i + first, 0))
    into = pl.BlockSpec((None, d, COLS), lambda i, j: (number, 0, j))
    out_of = pl.BlockSpec((None, COLS, d), lambda i, j: (number, j, 0))
    hidden = pl.BlockSpec((rows, COLS), lambda i, j: (i + first, j))
    extra = 1 if with_act else 0
    operands, specs, aliases = [h, dy, wg, wu, wd], [by_rows, by_rows, into, into, out_of], {}
    if so_far is not None:
        aliases = {len(operands) + i: i for i in range(len(so_far))}
        operands, specs = operands + so_far, specs + [pl.BlockSpec(memory_space=pl.ANY)] * len(so_far)
    return pl.pallas_call(
        functools.partial(gate_kernel, 3 + extra),
        grid=(tiles, ff // COLS),
        in_specs=specs,
        out_specs=[hidden, hidden, by_rows] + [hidden] * extra,
        out_shape=[shaped((tokens, ff)), shaped((tokens, ff)), shaped((tokens, d))] + [shaped((tokens, ff))] * extra,
        input_output_aliases=aliases,
        compiler_params=params("parallel", "arbitrary"),
        cost_estimate=cost(6 * tokens * d * ff // parts, h, h, h),
    )(*operands)


def states_kernel(h_ref, dy_ref, dg_ref, du_ref, wg_ref, wu_ref, *refs):
    out_ref = refs[-1]
    by_a = dot(dg_ref[...], wg_ref[...], (1, 1)) + dot(du_ref[...], wu_ref[...], (1, 1))
    by_a = by_a.astype(BF16).astype(F32)
    wide = h_ref[...].astype(F32)
    scale = norm_scale(wide)
    along = jnp.mean(by_a * wide, -1, keepdims=True)
    by_h = (by_a * scale - wide * (scale * scale * scale * along)).astype(BF16)
    out_ref[...] = (dy_ref[...].astype(F32) + by_h.astype(F32)).astype(BF16)


def states_backward(h, dy, dg, du, wg, wu, number, part=0, parts=1, so_far=None):
    tokens, d = h.shape
    ff = wg.shape[2]
    rows = min(tokens // parts, 512)
    tiles = tokens // rows // parts
    first = part * tiles
    by_rows = pl.BlockSpec((rows, d), lambda i: (i + first, 0))
    hidden = pl.BlockSpec((rows, ff), lambda i: (i + first, 0))
    into = pl.BlockSpec((None, d, ff), lambda i: (number, 0, 0))
    operands, specs, aliases = [h, dy, dg, du, wg, wu], [by_rows, by_rows, hidden, hidden, into, into], {}
    if so_far is not None:
        aliases = {len(operands): 0}
        operands, specs = operands + [so_far], specs + [pl.BlockSpec(memory_space=pl.ANY)]
    return pl.pallas_call(
        states_kernel,
        grid=(tiles,),
        in_specs=specs,
        out_specs=by_rows,
        out_shape=shaped((tokens, d)),
        input_output_aliases=aliases,
        compiler_params=params("parallel"),
        cost_estimate=cost(4 * tokens * d * ff // parts, h, h, h),
    )(*operands)


def weight_kernel(a_ref, b_ref, out_ref):
    out_ref[...] = dot(a_ref[...], b_ref[...], (0, 0)).astype(BF16)


def weight_gradient(a, b):
    tokens, m = a.shape
    n = b.shape[1]
    if n > m:
        grid = (n // COLS,)
        specs = [pl.BlockSpec((tokens, m), lambda j: (0, 0)), pl.BlockSpec((tokens, COLS), lambda j: (0, j))]
        out = pl.BlockSpec((m, COLS), lambda j: (0, j))
    else:
        grid = (m // COLS,)
        specs = [pl.BlockSpec((tokens, COLS), lambda j: (0, j)), pl.BlockSpec((tokens, n), lambda j: (0, 0))]
        out = pl.BlockSpec((COLS, n), lambda j: (j, 0))
    return pl.pallas_call(
        weight_kernel,
        grid=grid,
        in_specs=specs,
        out_specs=out,
        out_shape=shaped((m, n)),
        compiler_params=params("parallel"),
        cost_estimate=cost(2 * tokens * m * n, a, b),
    )(a, b)


def adamw(w_ref, m_ref, v_ref, g_ref, w_out, m_out, v_out):
    g = g_ref[...].astype(F32)
    m = 0.9 * m_ref[...] + 0.1 * g
    v = 0.95 * v_ref[...] + 0.05 * g * g
    step = m * lax.rsqrt(v + 1e-8) + 0.1 * w_ref[...].astype(F32)
    w_out[...] = (w_ref[...].astype(F32) - 0.02 * step).astype(BF16)
    m_out[...] = m
    v_out[...] = v


def adamw_kernel(ids_ref, gg, gu, gd0, gd1, *refs):
    ins, outs = refs[:9], refs[-9:]
    way = pl.program_id(0)

    def one(which, g_ref):
        adamw(ins[which], ins[3 + which], ins[6 + which], g_ref, outs[which], outs[3 + which], outs[6 + which])

    @pl.when(way == 0)
    def _():
        one(0, gg)
        one(2, gd0)

    @pl.when(way == 1)
    def _():
        one(1, gu)
        one(2, gd1)


def adamw_step(ids, pieces, arrays, so_far, number):
    gg, gu, gd0, _ = pieces
    whole = lambda g: pl.BlockSpec(g.shape, lambda way, ids: (0, 0))
    gate = pl.BlockSpec((None, *gg.shape), lambda way, ids: (number, ids[0], 0))
    up = pl.BlockSpec((None, *gu.shape), lambda way, ids: (number, ids[1], 0))
    down = pl.BlockSpec((None, *gd0.shape), lambda way, ids: (number, 2 * ids[way] + way, 0))
    nine = [gate, up, down] * 3
    in_specs = [whole(g) for g in pieces] + nine
    aliases = {}
    operands = [*pieces, *arrays]
    if so_far is not None:
        in_specs += [pl.BlockSpec(memory_space=pl.ANY)] * 9
        aliases = {1 + len(operands) + i: i for i in range(9)}
        operands += so_far
    return pl.pallas_call(
        adamw_kernel,
        grid_spec=pltpu.PrefetchScalarGridSpec(num_scalar_prefetch=1, grid=(2,), in_specs=in_specs, out_specs=nine),
        out_shape=[shaped(a.shape, a.dtype) for a in arrays],
        input_output_aliases=aliases,
        compiler_params=params("arbitrary"),
        cost_estimate=pl.CostEstimate(flops=4_000_000_000, bytes_accessed=22 * sum(g.size for g in pieces), transcendentals=0),
    )(ids, *operands)


class Reduce:
    def __init__(self, me, n, ways, local, way, parts, part):
        self.me, self.n, self.way, self.pairs = me, n, way, ways[way]
        self.parts, self.part, self.left = parts, part, n - 1
        self.slabs = local.reshape(n * parts, local.shape[0] // (n * parts), local.shape[1])
        self.value = self.own()

    def own(self):
        at = self.n - self.left
        chunk = lax.rem(self.me + 2 * self.n + (-at if self.way == 0 else at), self.n)
        return lax.dynamic_index_in_dim(self.slabs, chunk * self.parts + self.part, 0, False)

    def send(self):
        self.come = lax.ppermute(self.value, "dp", self.pairs)

    def receive(self):
        self.left -= 1
        self.value = (self.come.astype(F32) + self.own().astype(F32)).astype(BF16)


class Gather:
    def __init__(self, value, pairs):
        self.value, self.pairs = value, pairs

    def send(self):
        self.come = lax.ppermute(self.value, "dp", self.pairs)

    def receive(self):
        self.value = self.come


def solution(mesh):
    n = mesh.shape["dp"]
    ways = ([(i, (i + 1) % n) for i in range(n)], [(i, (i - 1) % n) for i in range(n)])

    def step(x, dy, *arrays):
        wg, wu, wd = arrays[:3]
        me = lax.axis_index("dp")

        def slot(rings, kernel):
            for ring in rings:
                ring.send()
            out = kernel()
            for ring in rings:
                ring.receive()
            return out

        def reduce(local, way, parts=1, part=0):
            return Reduce(me, n, ways, local, way, parts, part)

        def both(down):
            return [reduce(down, way, 2, way) for way in (0, 1)]

        def live(*rings):
            return [r for r in rings if r.left > 0]

        h0, by_y = x[0], dy[0]
        h1, a0, act0 = forward(h0, wg, wu, wd, 0)
        dg1, du1, a1, act1 = gate_backward(h1, by_y, wg, wu, wd, 1, True)
        down1 = weight_gradient(act1, by_y)
        rings = both(down1)
        gate1 = slot(live(*rings), lambda: weight_gradient(a1, dg1))
        rings.append(reduce(gate1, 0))
        up1 = slot(live(*rings), lambda: weight_gradient(a1, du1))
        rings.append(reduce(up1, 1))
        by_h = None
        for part in range(2):
            by_h = slot(live(*rings), lambda: states_backward(h1, by_y, dg1, du1, wg, wu, 1, part, 2, by_h))
        hidden = None
        for part in range(2):
            hidden = slot(live(*rings), lambda: list(gate_backward(h0, by_h, wg, wu, wd, 0, False, part, 2, hidden)))
        dg0, du0, _ = hidden
        down0 = slot(live(*rings), lambda: weight_gradient(act0, by_h))
        rings0 = both(down0)
        gate0 = slot(live(*rings, *rings0), lambda: weight_gradient(a0, dg0))
        rings0.append(reduce(gate0, 0))
        up0 = slot(live(*rings, *rings0), lambda: weight_gradient(a0, du0))
        rings0.append(reduce(up0, 1))

        def order(rings):
            return [rings[i] for i in (2, 3, 0, 1)]

        so_far = None
        for number, mine, others in ((1, rings, rings0), (0, rings0, [])):
            while live(*mine):
                slot(live(*mine), lambda: None)
            gathers = [Gather(r.value, ways[r.way]) for r in order(mine)]
            for s in range(n):
                ids = jnp.stack([lax.rem(me + n - s, n), lax.rem(me + s, n)])
                pieces = [g.value for g in gathers]
                ring_steps = live(*others) + (gathers if s < n - 1 else [])
                so_far = slot(ring_steps, lambda: list(adamw_step(ids, pieces, arrays, so_far, number)))
        return tuple(so_far)

    step = jax.shard_map(
        step,
        mesh=mesh,
        in_specs=(P(("rep", "dp"), None, None),) * 2 + (P(None, None, None),) * 9,
        out_specs=(P("rep", None, None),) * 9,
        check_vma=False,
    )
    return step
```

time: 548 us -> 562 us (1.026)
  the two profiles are of different devices: /device:TPU:21 before, /device:TPU:30 now
where the time goes in v1:
time: 562 us; the launch traced here: 553 us
  Pallas kernels  268 us (48%)
  starting transfers between devices  161 us (29%)
  waiting for transfers between devices  92.3 us (16%)
  other arithmetic  20.2 us (4%)
  local copies, waits for them, and re-layouts  9.86 us (2%)
    ppermute x112, starting transfers between devices, send(): self.come = lax.ppermute(self.value, 'dp', self.pairs)  161 us
    pallas_call x16, Pallas kernels, adamw_step(): pl.pallas_call(adamw_kernel, grid_spec=pltpu.PrefetchScalarGridSpec(num_s...  98.2 us
    ppermute x112, waiting for transfers between devices, send(): self.come = lax.ppermute(self.value, 'dp', self.pairs)  92.3 us
    pallas_call x6, Pallas kernels, weight_gradient(): pl.pallas_call(weight_kernel, grid=grid, in_specs=specs, out_specs=out, o...  64 us
    pallas_call x3, Pallas kernels, gate_backward(): pl.pallas_call(functools.partial(gate_kernel, 3 + extra), grid=(tiles, ff...  55.8 us
    pallas_call x1, Pallas kernels, forward(): pl.pallas_call(forward_kernel, grid=(tokens // rows, ff // COLS), in_spec...  26.9 us
    pallas_call x2, Pallas kernels, states_backward(): pl.pallas_call(states_kernel, grid=(tiles,), in_specs=specs, out_specs=by...  23.2 us
    convert_element_type x42, other arithmetic, receive(): self.value = (self.come.astype(F32) + self.own().astype(F32)).astype(BF16)  15.1 us
  transfers between devices with their start and end apart: 112, of which 36 were waited for; matrix products, arithmetic and copies ran while one was open for 5% of the time, Pallas kernels for 35%

profile of v1, /device:TPU:30, one launch (start us, length us, event | category | flops | bytes accessed | tf_op | source)
XLA Modules:
  0.0 553.2 jit_solution(8134380013686768862)
XLA Ops:
  0.7 26.9 %shard_map.178 = (bf16[2048,640]{1,0:T(8,128)(2,1)}, bf16[2048,640]{1,0:T(8,128)(2,1)}, bf16[2048,1792]{1,0:T(8,128)(2,1)}) custom-call(bf16[2048,640]{1,0:T(8,128)(2,1)} %bitcast.205, bf16[2,640,1792]{2,1,0:T(8,128)(2,1)} %refs_0_.31, bf16[2,640,1792]{2,1,0:T(8,128)(2,1)} %refs_1_.31, bf16[2,1792,640]{2,1,0:T(8,128)(2,1)} %refs_2_.31), custom_call_target="tpu_custom_call" | custom-call | flops 14092861440 | bytes 7864320 | tf_op jit(solution)/shard_map/pallas_call | solution.py:66
  27.5 27.6 %shard_map.179 = (bf16[2048,1792]{1,0:T(8,128)(2,1)}, bf16[2048,1792]{1,0:T(8,128)(2,1)}, bf16[2048,640]{1,0:T(8,128)(2,1)}, bf16[2048,1792]{1,0:T(8,128)(2,1)}) custom-call(bf16[2048,640]{1,0:T(8,128)(2,1)} %get-tuple-element.157.h_ref, bf16[2048,640]{1,0:T(8,128)(2,1)} %bitcast.201, bf16[2,640,1792]{2,1,0:T(8,128)(2,1)} %refs_0_.31, ...), custom_call_target="tpu_custom_call" | custom-call | flops 14092861440 | bytes 7864320 | tf_op jit(solution)/shard_map/pallas_call | solution.py:114
  55.2 11.0 %shard_map.189 = bf16[1792,640]{1,0:T(8,128)(2,1)} custom-call(bf16[2048,1792]{1,0:T(8,128)(2,1)} %get-tuple-element.167.a_ref, bf16[2048,640]{1,0:T(8,128)(2,1)} %bitcast.202), custom_call_target="tpu_custom_call" | custom-call | flops 4697620480 | bytes 9961472 | tf_op jit(solution)/shard_map/pallas_call | solution.py:177
  67.9 7.3 %collective-permute-start.98 = (bf16[112,640]{1,0:T(8,128)(2,1)}, bf16[112,640]{1,0:T(8,128)(2,1)}, u32[]{:S(2)}, u32[]{:S(2)}) collective-permute-start(bf16[112,640]{1,0:T(8,128)(2,1)} %get-tuple-element.317), channel_id=1, source_target_pairs={{0,7},{1,0},{2,1},{3,2},{4,3},{5,4},{6,5},{7,6},{8,15},{9,8},{10,9... | collective-permute-start | bytes 430088 | tf_op jit(solution)/shard_map/ppermute | solution.py:253
  75.2 10.5 %shard_map.187 = bf16[640,1792]{1,0:T(8,128)(2,1)} custom-call(bf16[2048,640]{1,0:T(8,128)(2,1)} %get-tuple-element.166.a_ref, bf16[2048,1792]{1,0:T(8,128)(2,1)} %get-tuple-element.158.dg_ref.b_ref), custom_call_target="tpu_custom_call" | custom-call | flops 4697620480 | bytes 9961472 | tf_op jit(solution)/shard_map/pallas_call | solution.py:177
  86.8 10.5 %shard_map.188 = bf16[640,1792]{1,0:T(8,128)(2,1)} custom-call(bf16[2048,640]{1,0:T(8,128)(2,1)} %get-tuple-element.166.a_ref, bf16[2048,1792]{1,0:T(8,128)(2,1)} %get-tuple-element.159.du_ref.b_ref), custom_call_target="tpu_custom_call" | custom-call | flops 4697620480 | bytes 9961472 | tf_op jit(solution)/shard_map/pallas_call | solution.py:177
  98.3 3.8 collective-permute-start.70
  102.1 11.6 %shard_map.180.refs_0_ = bf16[2048,640]{1,0:T(8,128)(2,1)} custom-call(bf16[2048,640]{1,0:T(8,128)(2,1)} %get-tuple-element.157.h_ref, bf16[2048,640]{1,0:T(8,128)(2,1)} %bitcast.203, bf16[2048,1792]{1,0:T(8,128)(2,1)} %get-tuple-element.158.dg_ref.b_ref, bf16[2048,1792]{1,0:T(8,128)(2,1)} %get-tuple-element.159.du_ref.b_ref, ...), custom_call_target="tpu_custom_call" | custom-call | flops 4697620480 | bytes 7864320 | tf_op jit(solution)/shard_map/pallas_call | solution.py:150
  113.6 11.6 %shard_map.181.dy_ref.b_ref = bf16[2048,640]{1,0:T(8,128)(2,1)} custom-call(bf16[2048,640]{1,0:T(8,128)(2,1)} %get-tuple-element.157.h_ref, bf16[2048,640]{1,0:T(8,128)(2,1)} %bitcast.204, bf16[2048,1792]{1,0:T(8,128)(2,1)} %get-tuple-element.158.dg_ref.b_ref, bf16[2048,1792]{1,0:T(8,128)(2,1)} %get-tuple-element.159.du_ref.b_ref, ...), custom_call_target="tpu_custom_call", output_to_operand_aliasing={{}: (6, {})} | custom-call | flops 4697620480 | bytes 7864320 | tf_op jit(solution)/shard_map/pallas_call | solution.py:150
  125.2 11.0 %shard_map.186 = bf16[1792,640]{1,0:T(8,128)(2,1)} custom-call(bf16[2048,1792]{1,0:T(8,128)(2,1)} %get-tuple-element.165.a_ref, bf16[2048,640]{1,0:T(8,128)(2,1)} %shard_map.181.dy_ref.b_ref), custom_call_target="tpu_custom_call" | custom-call | flops 4697620480 | bytes 9961472 | tf_op jit(solution)/shard_map/pallas_call | solution.py:177
  143.8 14.1 %shard_map.182 = (bf16[2048,1792]{1,0:T(8,128)(2,1)}, bf16[2048,1792]{1,0:T(8,128)(2,1)}, bf16[2048,640]{1,0:T(8,128)(2,1)}) custom-call(bf16[2048,640]{1,0:T(8,128)(2,1)} %bitcast.206, bf16[2048,640]{1,0:T(8,128)(2,1)} %shard_map.181.dy_ref.b_ref, bf16[2,640,1792]{2,1,0:T(8,128)(2,1)} %refs_0_.31, bf16[2,640,1792]{2,1,0:T(8,128)(2,1)} %refs_1_.31, ...), custom_call_target="tpu_custom_call" | custom-call | flops 7046430720 | bytes 7864320 | tf_op jit(solution)/shard_map/pallas_call | solution.py:114
  157.8 14.1 %shard_map.183 = (bf16[2048,1792]{1,0:T(8,128)(2,1)}, bf16[2048,1792]{1,0:T(8,128)(2,1)}, bf16[2048,640]{1,0:T(8,128)(2,1)}) custom-call(bf16[2048,640]{1,0:T(8,128)(2,1)} %bitcast.207, bf16[2048,640]{1,0:T(8,128)(2,1)} %shard_map.181.dy_ref.b_ref, bf16[2,640,1792]{2,1,0:T(8,128)(2,1)} %refs_0_.31, ...), custom_call_target="tpu_custom_call", output_to_operand_aliasing={{0}: (5, {}), {1}: (6, {}), {2}: (7, {})} | custom-call | flops 7046430720 | bytes 7864320 | tf_op jit(solution)/shard_map/pallas_call | solution.py:114
  171.9 10.5 %shard_map.184 = bf16[640,1792]{1,0:T(8,128)(2,1)} custom-call(bf16[2048,640]{1,0:T(8,128)(2,1)} %get-tuple-element.156.a_ref, bf16[2048,1792]{1,0:T(8,128)(2,1)} %get-tuple-element.163.b_ref), custom_call_target="tpu_custom_call" | custom-call | flops 4697620480 | bytes 9961472 | tf_op jit(solution)/shard_map/pallas_call | solution.py:177
  182.4 10.5 %shard_map.185 = bf16[640,1792]{1,0:T(8,128)(2,1)} custom-call(bf16[2048,640]{1,0:T(8,128)(2,1)} %get-tuple-element.156.a_ref, bf16[2048,1792]{1,0:T(8,128)(2,1)} %get-tuple-element.164.b_ref), custom_call_target="tpu_custom_call" | custom-call | flops 4697620480 | bytes 9961472 | tf_op jit(solution)/shard_map/pallas_call | solution.py:177
  239.4 3.7 collective-permute-start.45
  245.3 3.3 collective-permute-start.102
  249.0 3.9 collective-permute-done.31
  259.4 4.1 collective-permute-done.46
  271.2 3.4 collective-permute-start.47
  291.2 4.5 collective-permute-done.48
  303.8 3.7 collective-permute-start.74
  307.6 4.7 collective-permute-done.74
  312.3 3.7 collective-permute-start.18
  334.6 3.6 collective-permute-start.75
  338.2 5.1 collective-permute-done.75
  343.4 3.7 collective-permute-start.19
  365.4 4.5 collective-permute-done.76
  373.2 4.1 collective-permute-done.20
  377.4 8.7 %collective-permute-done.62 = bf16[80,1792]{1,0:T(8,128)(2,1)S(1)} collective-permute-done((bf16[80,1792]{1,0:T(8,128)(2,1)S(1)}, bf16[80,1792]{1,0:T(8,128)(2,1)S(1)}, u32[]{:S(2)}, u32[]{:S(2)}) %collective-permute-start.62) | collective-permute-done | bytes 286752 | tf_op jit(solution)/shard_map/ppermute | solution.py:253
  386.2 10.8 %collective-permute-done.6 = bf16[80,1792]{1,0:T(8,128)(2,1)S(1)} collective-permute-done((bf16[80,1792]{1,0:T(8,128)(2,1)S(1)}, bf16[80,1792]{1,0:T(8,128)(2,1)S(1)}, u32[]{:S(2)}, u32[]{:S(2)}) %collective-permute-start.6) | collective-permute-done | bytes 286752 | tf_op jit(solution)/shard_map/ppermute | solution.py:253
  400.6 6.1 %shard_map.190 = (bf16[2,640,1792]{2,1,0:T(8,128)(2,1)}, bf16[2,640,1792]{2,1,0:T(8,128)(2,1)}, bf16[2,1792,640]{2,1,0:T(8,128)(2,1)}, f32[2,640,1792]{2,1,0:T(8...) custom-call(s32[2]{0:T(128)} %pad_add_fusion.7.ids_ref, ...), custom_call_target="tpu_custom_call" | custom-call | flops 4000000000 | bytes 9461760 | tf_op jit(solution)/shard_map/pallas_call | solution.py:230
  412.4 6.1 %shard_map.191 = (bf16[2,640,1792]{2,1,0:T(8,128)(2,1)}, bf16[2,640,1792]{2,1,0:T(8,128)(2,1)}, bf16[2,1792,640]{2,1,0:T(8,128)(2,1)}, f32[2,640,1792]{2,1,0:T(8...) custom-call(s32[2]{0:T(128)} %pad_add_fusion.6.ids_ref, ...), custom_call_target="tpu_custom_call", output_to_operand_aliasing={{0}: (14, {}), {1}: (15, {}), {2}: (16, {}), {3}: (17, {}),... | custom-call | flops 4000000000 | bytes 9461760 | tf_op jit(solution)/shard_map/pallas_call | solution.py:230
  426.5 6.1 %shard_map.192 = (bf16[2,640,1792]{2,1,0:T(8,128)(2,1)}, bf16[2,640,1792]{2,1,0:T(8,128)(2,1)}, bf16[2,1792,640]{2,1,0:T(8,128)(2,1)}, f32[2,640,1792]{2,1,0:T(8...) custom-call(s32[2]{0:T(128)} %pad_add_fusion.5.ids_ref, ...), custom_call_target="tpu_custom_call", output_to_operand_aliasing={{0}: (14, {}), {1}: (15, {}), {2}: (16, {}), {3}: (17, {}),... | custom-call | flops 4000000000 | bytes 9461760 | tf_op jit(solution)/shard_map/pallas_call | solution.py:230
  435.7 3.5 collective-permute-done.65.gg
  442.5 6.1 %shard_map.193 = (bf16[2,640,1792]{2,1,0:T(8,128)(2,1)}, bf16[2,640,1792]{2,1,0:T(8,128)(2,1)}, bf16[2,1792,640]{2,1,0:T(8,128)(2,1)}, f32[2,640,1792]{2,1,0:T(8...) custom-call(s32[2]{0:T(128)} %pad_add_fusion.4.ids_ref, ...), custom_call_target="tpu_custom_call", output_to_operand_aliasing={{0}: (14, {}), {1}: (15, {}), {2}: (16, {}), {3}: (17, {}),... | custom-call | flops 4000000000 | bytes 9461760 | tf_op jit(solution)/shard_map/pallas_call | solution.py:230
  455.3 6.2 %shard_map.194 = (bf16[2,640,1792]{2,1,0:T(8,128)(2,1)}, bf16[2,640,1792]{2,1,0:T(8,128)(2,1)}, bf16[2,1792,640]{2,1,0:T(8,128)(2,1)}, f32[2,640,1792]{2,1,0:T(8...) custom-call(s32[2]{0:T(128)} %pad_add_fusion.3.ids_ref, ...), custom_call_target="tpu_custom_call", output_to_operand_aliasing={{0}: (14, {}), {1}: (15, {}), {2}: (16, {}), {3}: (17, {}),... | custom-call | flops 4000000000 | bytes 9461760 | tf_op jit(solution)/shard_map/pallas_call | solution.py:230
  465.6 3.4 collective-permute-done.67.gg
  472.3 6.1 %shard_map.195 = (bf16[2,640,1792]{2,1,0:T(8,128)(2,1)}, bf16[2,640,1792]{2,1,0:T(8,128)(2,1)}, bf16[2,1792,640]{2,1,0:T(8,128)(2,1)}, f32[2,640,1792]{2,1,0:T(8...) custom-call(s32[2]{0:T(128)} %pad_add_fusion.2.ids_ref, ...), custom_call_target="tpu_custom_call", output_to_operand_aliasing={{0}: (14, {}), {1}: (15, {}), {2}: (16, {}), {3}: (17, {}),... | custom-call | flops 4000000000 | bytes 9461760 | tf_op jit(solution)/shard_map/pallas_call | solution.py:230
  485.1 6.1 %shard_map.196 = (bf16[2,640,1792]{2,1,0:T(8,128)(2,1)}, bf16[2,640,1792]{2,1,0:T(8,128)(2,1)}, bf16[2,1792,640]{2,1,0:T(8,128)(2,1)}, f32[2,640,1792]{2,1,0:T(8...) custom-call(s32[2]{0:T(128)} %pad_add_fusion.1.ids_ref, ...), custom_call_target="tpu_custom_call", output_to_operand_aliasing={{0}: (14, {}), {1}: (15, {}), {2}: (16, {}), {3}: (17, {}),... | custom-call | flops 4000000000 | bytes 9461760 | tf_op jit(solution)/shard_map/pallas_call | solution.py:230
  497.5 6.1 %shard_map.197 = (bf16[2,640,1792]{2,1,0:T(8,128)(2,1)}, bf16[2,640,1792]{2,1,0:T(8,128)(2,1)}, bf16[2,1792,640]{2,1,0:T(8,128)(2,1)}, f32[2,640,1792]{2,1,0:T(8...) custom-call(s32[2]{0:T(128)} %pad_add_fusion.ids_ref, ...), custom_call_target="tpu_custom_call", output_to_operand_aliasing={{0}: (14, {}), {1}: (15, {}), {2}: (16, {}), {3}: (17, {}),... | custom-call | flops 4000000000 | bytes 9461760 | tf_op jit(solution)/shard_map/pallas_call | solution.py:230
  503.6 6.2 %shard_map.198 = (bf16[2,640,1792]{2,1,0:T(8,128)(2,1)}, bf16[2,640,1792]{2,1,0:T(8,128)(2,1)}, bf16[2,1792,640]{2,1,0:T(8,128)(2,1)}, f32[2,640,1792]{2,1,0:T(8...) custom-call(s32[2]{0:T(128)} %pad_add_fusion.7.ids_ref, ...), custom_call_target="tpu_custom_call", output_to_operand_aliasing={{0}: (14, {}), {1}: (15, {}), {2}: (16, {}), {3}: (17, {}),... | custom-call | flops 4000000000 | bytes 9461760 | tf_op jit(solution)/shard_map/pallas_call | solution.py:230
  509.8 6.2 %shard_map.199 = (bf16[2,640,1792]{2,1,0:T(8,128)(2,1)}, bf16[2,640,1792]{2,1,0:T(8,128)(2,1)}, bf16[2,1792,640]{2,1,0:T(8,128)(2,1)}, f32[2,640,1792]{2,1,0:T(8...) custom-call(s32[2]{0:T(128)} %pad_add_fusion.6.ids_ref, ...), custom_call_target="tpu_custom_call", output_to_operand_aliasing={{0}: (14, {}), {1}: (15, {}), {2}: (16, {}), {3}: (17, {}),... | custom-call | flops 4000000000 | bytes 9461760 | tf_op jit(solution)/shard_map/pallas_call | solution.py:230
  515.9 6.2 %shard_map.200 = (bf16[2,640,1792]{2,1,0:T(8,128)(2,1)}, bf16[2,640,1792]{2,1,0:T(8,128)(2,1)}, bf16[2,1792,640]{2,1,0:T(8,128)(2,1)}, f32[2,640,1792]{2,1,0:T(8...) custom-call(s32[2]{0:T(128)} %pad_add_fusion.5.ids_ref, ...), custom_call_target="tpu_custom_call", output_to_operand_aliasing={{0}: (14, {}), {1}: (15, {}), {2}: (16, {}), {3}: (17, {}),... | custom-call | flops 4000000000 | bytes 9461760 | tf_op jit(solution)/shard_map/pallas_call | solution.py:230
  522.1 6.2 %shard_map.201 = (bf16[2,640,1792]{2,1,0:T(8,128)(2,1)}, bf16[2,640,1792]{2,1,0:T(8,128)(2,1)}, bf16[2,1792,640]{2,1,0:T(8,128)(2,1)}, f32[2,640,1792]{2,1,0:T(8...) custom-call(s32[2]{0:T(128)} %pad_add_fusion.4.ids_ref, ...), custom_call_target="tpu_custom_call", output_to_operand_aliasing={{0}: (14, {}), {1}: (15, {}), {2}: (16, {}), {3}: (17, {}),... | custom-call | flops 4000000000 | bytes 9461760 | tf_op jit(solution)/shard_map/pallas_call | solution.py:230
  528.2 6.2 %shard_map.202 = (bf16[2,640,1792]{2,1,0:T(8,128)(2,1)}, bf16[2,640,1792]{2,1,0:T(8,128)(2,1)}, bf16[2,1792,640]{2,1,0:T(8,128)(2,1)}, f32[2,640,1792]{2,1,0:T(8...) custom-call(s32[2]{0:T(128)} %pad_add_fusion.3.ids_ref, ...), custom_call_target="tpu_custom_call", output_to_operand_aliasing={{0}: (14, {}), {1}: (15, {}), {2}: (16, {}), {3}: (17, {}),... | custom-call | flops 4000000000 | bytes 9461760 | tf_op jit(solution)/shard_map/pallas_call | solution.py:230
  534.4 6.2 %shard_map.203 = (bf16[2,640,1792]{2,1,0:T(8,128)(2,1)}, bf16[2,640,1792]{2,1,0:T(8,128)(2,1)}, bf16[2,1792,640]{2,1,0:T(8,128)(2,1)}, f32[2,640,1792]{2,1,0:T(8...) custom-call(s32[2]{0:T(128)} %pad_add_fusion.2.ids_ref, ...), custom_call_target="tpu_custom_call", output_to_operand_aliasing={{0}: (14, {}), {1}: (15, {}), {2}: (16, {}), {3}: (17, {}),... | custom-call | flops 4000000000 | bytes 9461760 | tf_op jit(solution)/shard_map/pallas_call | solution.py:230
  540.6 6.2 %shard_map.204 = (bf16[2,640,1792]{2,1,0:T(8,128)(2,1)}, bf16[2,640,1792]{2,1,0:T(8,128)(2,1)}, bf16[2,1792,640]{2,1,0:T(8,128)(2,1)}, f32[2,640,1792]{2,1,0:T(8...) custom-call(s32[2]{0:T(128)} %pad_add_fusion.1.ids_ref, ...), custom_call_target="tpu_custom_call", output_to_operand_aliasing={{0}: (14, {}), {1}: (15, {}), {2}: (16, {}), {3}: (17, {}),... | custom-call | flops 4000000000 | bytes 9461760 | tf_op jit(solution)/shard_map/pallas_call | solution.py:230
  546.8 6.2 %shard_map.205 = (bf16[2,640,1792]{2,1,0:T(8,128)(2,1)}, bf16[2,640,1792]{2,1,0:T(8,128)(2,1)}, bf16[2,1792,640]{2,1,0:T(8,128)(2,1)}, f32[2,640,1792]{2,1,0:T(8...) custom-call(s32[2]{0:T(128)} %pad_add_fusion.ids_ref, ...), custom_call_target="tpu_custom_call", output_to_operand_aliasing={{0}: (14, {}), {1}: (15, {}), {2}: (16, {}), {3}: (17, {}),... | custom-call | flops 4000000000 | bytes 9461760 | tf_op jit(solution)/shard_map/pallas_call | solution.py:230
  (382 shorter events, 189.5 us)
Async XLA Ops:
  67.9 129.8 %collective-permute-start.98 = (bf16[112,640]{1,0:T(8,128)(2,1)}, bf16[112,640]{1,0:T(8,128)(2,1)}, u32[]{:S(2)}, u32[]{:S(2)}) collective-permute-start(bf16[112,640]{1,0:T(8,128)(2,1)} %get-tuple-element.317), channel_id=1, source_target_pairs={{0,7},{1,0},{2,1},{3,2},{4,3},{5,4},{6,5},{7,6},{8,15},{9,8},{10,9... | collective-permute-start | bytes 430088 | tf_op jit(solution)/shard_map/ppermute | solution.py:253
  75.2 122.6 %collective-permute-start.84 = (bf16[112,640]{1,0:T(8,128)(2,1)}, bf16[112,640]{1,0:T(8,128)(2,1)}, u32[]{:S(2)}, u32[]{:S(2)}) collective-permute-start(bf16[112,640]{1,0:T(8,128)(2,1)} %get-tuple-element.318), channel_id=1, source_target_pairs={{0,1},{1,2},{2,3},{3,4},{4,5},{5,6},{6,7},{7,0},{8,9},{9,10},{10,1... | collective-permute-start | bytes 430088 | tf_op jit(solution)/shard_map/ppermute | solution.py:253
  86.6 132.4 %collective-permute-start.56 = (bf16[80,1792]{1,0:T(8,128)(2,1)S(1)}, bf16[80,1792]{1,0:T(8,128)(2,1)S(1)}, u32[]{:S(2)}, u32[]{:S(2)}) collective-permute-start(bf16[80,1792]{1,0:T(8,128)(2,1)S(1)} %dynamic-slice_bitcast_fusion.1), channel_id=1, source_target_pairs={{0,1},{1,2},{2,3},{3,4},{4,5},{5,6},{6,7},{7,0},{8,9},{9,10},{10,1... | collective-permute-start | bytes 860168 | tf_op jit(solution)/shard_map/ppermute | solution.py:253
  98.3 108.5 %collective-permute-start.70 = (bf16[80,1792]{1,0:T(8,128)(2,1)S(1)}, bf16[80,1792]{1,0:T(8,128)(2,1)S(1)}, u32[]{:S(2)}, u32[]{:S(2)}) collective-permute-start(bf16[80,1792]{1,0:T(8,128)(2,1)S(1)} %dynamic-slice_bitcast_fusion), channel_id=1, source_target_pairs={{0,7},{1,0},{2,1},{3,2},{4,3},{5,4},{6,5},{7,6},{8,15},{9,8},{10,9... | collective-permute-start | bytes 860168 | tf_op jit(solution)/shard_map/ppermute | solution.py:253
  137.9 64.2 %collective-permute-start.42 = (bf16[112,640]{1,0:T(8,128)(2,1)}, bf16[112,640]{1,0:T(8,128)(2,1)}, u32[]{:S(2)}, u32[]{:S(2)}) collective-permute-start(bf16[112,640]{1,0:T(8,128)(2,1)} %get-tuple-element.333), channel_id=1, source_target_pairs={{0,7},{1,0},{2,1},{3,2},{4,3},{5,4},{6,5},{7,6},{8,15},{9,8},{10,9... | collective-permute-start | bytes 430088 | tf_op jit(solution)/shard_map/ppermute | solution.py:253
  197.8 16.9 %collective-permute-start.14 = (bf16[80,1792]{1,0:T(8,128)(2,1)}, bf16[80,1792]{1,0:T(8,128)(2,1)S(1)}, u32[]{:S(2)}, u32[]{:S(2)}) collective-permute-start(bf16[80,1792]{1,0:T(8,128)(2,1)} %dynamic-slice_bitcast_fusion.2), channel_id=1, source_target_pairs={{0,7},{1,0},{2,1},{3,2},{4,3},{5,4},{6,5},{7,6},{8,15},{9,8},{10,9... | collective-permute-start | bytes 860168 | tf_op jit(solution)/shard_map/ppermute | solution.py:253
  202.2 21.6 %collective-permute-start = (bf16[80,1792]{1,0:T(8,128)(2,1)}, bf16[80,1792]{1,0:T(8,128)(2,1)S(1)}, u32[]{:S(2)}, u32[]{:S(2)}) collective-permute-start(bf16[80,1792]{1,0:T(8,128)(2,1)} %dynamic-slice_bitcast_fusion.3), channel_id=1, source_target_pairs={{0,1},{1,2},{2,3},{3,4},{4,5},{5,6},{6,7},{7,0},{8,9},{9,10},{10,1... | collective-permute-start | bytes 860168 | tf_op jit(solution)/shard_map/ppermute | solution.py:253
  219.3 29.4 %collective-permute-start.57 = (bf16[80,1792]{1,0:T(8,128)(2,1)S(1)}, bf16[80,1792]{1,0:T(8,128)(2,1)S(1)}, u32[]{:S(2)}, u32[]{:S(2)}) collective-permute-start(bf16[80,1792]{1,0:T(8,128)(2,1)S(1)} %fusion.13), channel_id=1, source_target_pairs={{0,1},{1,2},{2,3},{3,4},{4,5},{5,6},{6,7},{7,0},{8,9},{9,10},{10,1... | collective-permute-start | bytes 860168 | tf_op jit(solution)/shard_map/ppermute | solution.py:253
  219.9 17.9 %collective-permute-start.71 = (bf16[80,1792]{1,0:T(8,128)(2,1)S(1)}, bf16[80,1792]{1,0:T(8,128)(2,1)S(1)}, u32[]{:S(2)}, u32[]{:S(2)}) collective-permute-start(bf16[80,1792]{1,0:T(8,128)(2,1)S(1)} %fusion.6), channel_id=1, source_target_pairs={{0,7},{1,0},{2,1},{3,2},{4,3},{5,4},{6,5},{7,6},{8,15},{9,8},{10,9... | collective-permute-start | bytes 860168 | tf_op jit(solution)/shard_map/ppermute | solution.py:253
  226.7 18.6 %collective-permute-start.15 = (bf16[80,1792]{1,0:T(8,128)(2,1)S(1)}, bf16[80,1792]{1,0:T(8,128)(2,1)S(1)}, u32[]{:S(2)}, u32[]{:S(2)}) collective-permute-start(bf16[80,1792]{1,0:T(8,128)(2,1)S(1)} %fusion.20), channel_id=1, source_target_pairs={{0,7},{1,0},{2,1},{3,2},{4,3},{5,4},{6,5},{7,6},{8,15},{9,8},{10,9... | collective-permute-start | bytes 860168 | tf_op jit(solution)/shard_map/ppermute | solution.py:253
  233.0 22.1 %collective-permute-start.1 = (bf16[80,1792]{1,0:T(8,128)(2,1)S(1)}, bf16[80,1792]{1,0:T(8,128)(2,1)S(1)}, u32[]{:S(2)}, u32[]{:S(2)}) collective-permute-start(bf16[80,1792]{1,0:T(8,128)(2,1)S(1)} %fusion.27), channel_id=1, source_target_pairs={{0,1},{1,2},{2,3},{3,4},{4,5},{5,6},{6,7},{7,0},{8,9},{9,10},{10,1... | collective-permute-start | bytes 860168 | tf_op jit(solution)/shard_map/ppermute | solution.py:253
  248.9 32.0 %collective-permute-start.58 = (bf16[80,1792]{1,0:T(8,128)(2,1)S(1)}, bf16[80,1792]{1,0:T(8,128)(2,1)S(1)}, u32[]{:S(2)}, u32[]{:S(2)}) collective-permute-start(bf16[80,1792]{1,0:T(8,128)(2,1)S(1)} %fusion.12), channel_id=1, source_target_pairs={{0,1},{1,2},{2,3},{3,4},{4,5},{5,6},{6,7},{7,0},{8,9},{9,10},{10,1... | collective-permute-start | bytes 860168 | tf_op jit(solution)/shard_map/ppermute | solution.py:253
  252.9 14.9 %collective-permute-start.72 = (bf16[80,1792]{1,0:T(8,128)(2,1)S(1)}, bf16[80,1792]{1,0:T(8,128)(2,1)S(1)}, u32[]{:S(2)}, u32[]{:S(2)}) collective-permute-start(bf16[80,1792]{1,0:T(8,128)(2,1)S(1)} %fusion.5), channel_id=1, source_target_pairs={{0,7},{1,0},{2,1},{3,2},{4,3},{5,4},{6,5},{7,6},{8,15},{9,8},{10,9... | collective-permute-start | bytes 860168 | tf_op jit(solution)/shard_map/ppermute | solution.py:253
  257.4 20.1 %collective-permute-start.16 = (bf16[80,1792]{1,0:T(8,128)(2,1)S(1)}, bf16[80,1792]{1,0:T(8,128)(2,1)S(1)}, u32[]{:S(2)}, u32[]{:S(2)}) collective-permute-start(bf16[80,1792]{1,0:T(8,128)(2,1)S(1)} %fusion.19), channel_id=1, source_target_pairs={{0,7},{1,0},{2,1},{3,2},{4,3},{5,4},{6,5},{7,6},{8,15},{9,8},{10,9... | collective-permute-start | bytes 860168 | tf_op jit(solution)/shard_map/ppermute | solution.py:253
  263.5 22.2 %collective-permute-start.2 = (bf16[80,1792]{1,0:T(8,128)(2,1)S(1)}, bf16[80,1792]{1,0:T(8,128)(2,1)S(1)}, u32[]{:S(2)}, u32[]{:S(2)}) collective-permute-start(bf16[80,1792]{1,0:T(8,128)(2,1)S(1)} %fusion.26), channel_id=1, source_target_pairs={{0,1},{1,2},{2,3},{3,4},{4,5},{5,6},{6,7},{7,0},{8,9},{9,10},{10,1... | collective-permute-start | bytes 860168 | tf_op jit(solution)/shard_map/ppermute | solution.py:253
  281.2 22.4 %collective-permute-start.59 = (bf16[80,1792]{1,0:T(8,128)(2,1)S(1)}, bf16[80,1792]{1,0:T(8,128)(2,1)S(1)}, u32[]{:S(2)}, u32[]{:S(2)}) collective-permute-start(bf16[80,1792]{1,0:T(8,128)(2,1)S(1)} %fusion.11), channel_id=1, source_target_pairs={{0,1},{1,2},{2,3},{3,4},{4,5},{5,6},{6,7},{7,0},{8,9},{9,10},{10,1... | collective-permute-start | bytes 860168 | tf_op jit(solution)/shard_map/ppermute | solution.py:253
  283.7 16.2 %collective-permute-start.73 = (bf16[80,1792]{1,0:T(8,128)(2,1)S(1)}, bf16[80,1792]{1,0:T(8,128)(2,1)S(1)}, u32[]{:S(2)}, u32[]{:S(2)}) collective-permute-start(bf16[80,1792]{1,0:T(8,128)(2,1)S(1)} %fusion.4), channel_id=1, source_target_pairs={{0,7},{1,0},{2,1},{3,2},{4,3},{5,4},{6,5},{7,6},{8,15},{9,8},{10,9... | collective-permute-start | bytes 860168 | tf_op jit(solution)/shard_map/ppermute | solution.py:253
  296.2 19.9 %collective-permute-start.105 = (bf16[112,640]{1,0:T(8,128)(2,1)S(1)}, bf16[112,640]{1,0:T(8,128)(2,1)S(1)}, u32[]{:S(2)}, u32[]{:S(2)}) collective-permute-start(bf16[112,640]{1,0:T(8,128)(2,1)S(1)} %get-tuple-element.303.gd1), channel_id=1, source_target_pairs={{0,7},{1,0},{2,1},{3,2},{4,3},{5,4},{6,5},{7,6},{8,15},{9,8},{10,9... | collective-permute-start | bytes 430088 | tf_op jit(solution)/shard_map/ppermute | solution.py:265
  300.0 16.2 %collective-permute-start.91 = (bf16[112,640]{1,0:T(8,128)(2,1)S(1)}, bf16[112,640]{1,0:T(8,128)(2,1)S(1)}, u32[]{:S(2)}, u32[]{:S(2)}) collective-permute-start(bf16[112,640]{1,0:T(8,128)(2,1)S(1)} %get-tuple-element.304.gd0), channel_id=1, source_target_pairs={{0,1},{1,2},{2,3},{3,4},{4,5},{5,6},{6,7},{7,0},{8,9},{9,10},{10,1... | collective-permute-start | bytes 430088 | tf_op jit(solution)/shard_map/ppermute | solution.py:265
  300.2 19.2 %collective-permute-start.49 = (bf16[112,640]{1,0:T(8,128)(2,1)S(1)}, bf16[112,640]{1,0:T(8,128)(2,1)S(1)}, u32[]{:S(2)}, u32[]{:S(2)}) collective-permute-start(bf16[112,640]{1,0:T(8,128)(2,1)S(1)} %get-tuple-element.319.gd1), channel_id=1, source_target_pairs={{0,7},{1,0},{2,1},{3,2},{4,3},{5,4},{6,5},{7,6},{8,15},{9,8},{10,9... | collective-permute-start | bytes 430088 | tf_op jit(solution)/shard_map/ppermute | solution.py:265
  303.6 15.9 %collective-permute-start.35 = (bf16[112,640]{1,0:T(8,128)(2,1)S(1)}, bf16[112,640]{1,0:T(8,128)(2,1)S(1)}, u32[]{:S(2)}, u32[]{:S(2)}) collective-permute-start(bf16[112,640]{1,0:T(8,128)(2,1)S(1)} %get-tuple-element.320.gd0), channel_id=1, source_target_pairs={{0,1},{1,2},{2,3},{3,4},{4,5},{5,6},{6,7},{7,0},{8,9},{9,10},{10,1... | collective-permute-start | bytes 430088 | tf_op jit(solution)/shard_map/ppermute | solution.py:265
  316.1 15.8 %collective-permute-start.60 = (bf16[80,1792]{1,0:T(8,128)(2,1)S(1)}, bf16[80,1792]{1,0:T(8,128)(2,1)S(1)}, u32[]{:S(2)}, u32[]{:S(2)}) collective-permute-start(bf16[80,1792]{1,0:T(8,128)(2,1)S(1)} %fusion.10), channel_id=1, source_target_pairs={{0,1},{1,2},{2,3},{3,4},{4,5},{5,6},{6,7},{7,0},{8,9},{9,10},{10,1... | collective-permute-start | bytes 860168 | tf_op jit(solution)/shard_map/ppermute | solution.py:253
  325.8 21.4 %collective-permute-start.107 = (bf16[112,640]{1,0:T(8,128)(2,1)S(1)}, bf16[112,640]{1,0:T(8,128)(2,1)S(1)}, u32[]{:S(2)}, u32[]{:S(2)}) collective-permute-start(bf16[112,640]{1,0:T(8,128)(2,1)S(1)} %collective-permute-done.106.gd1), channel_id=1, source_target_pairs={{0,7},{1,0},{2,1},{3,2},{4,3},{5,4},{6,5},{7,6},{8,15},{9,8},{10,9... | collective-permute-start | bytes 430088 | tf_op jit(solution)/shard_map/ppermute | solution.py:265
  328.6 18.7 %collective-permute-start.93 = (bf16[112,640]{1,0:T(8,128)(2,1)S(1)}, bf16[112,640]{1,0:T(8,128)(2,1)S(1)}, u32[]{:S(2)}, u32[]{:S(2)}) collective-permute-start(bf16[112,640]{1,0:T(8,128)(2,1)S(1)} %collective-permute-done.92.gd0), channel_id=1, source_target_pairs={{0,1},{1,2},{2,3},{3,4},{4,5},{5,6},{6,7},{7,0},{8,9},{9,10},{10,1... | collective-permute-start | bytes 430088 | tf_op jit(solution)/shard_map/ppermute | solution.py:265
  329.2 21.4 %collective-permute-start.51 = (bf16[112,640]{1,0:T(8,128)(2,1)S(1)}, bf16[112,640]{1,0:T(8,128)(2,1)S(1)}, u32[]{:S(2)}, u32[]{:S(2)}) collective-permute-start(bf16[112,640]{1,0:T(8,128)(2,1)S(1)} %collective-permute-done.50.gd1), channel_id=1, source_target_pairs={{0,7},{1,0},{2,1},{3,2},{4,3},{5,4},{6,5},{7,6},{8,15},{9,8},{10,9... | collective-permute-start | bytes 430088 | tf_op jit(solution)/shard_map/ppermute | solution.py:265
  331.9 18.8 %collective-permute-start.37 = (bf16[112,640]{1,0:T(8,128)(2,1)S(1)}, bf16[112,640]{1,0:T(8,128)(2,1)S(1)}, u32[]{:S(2)}, u32[]{:S(2)}) collective-permute-start(bf16[112,640]{1,0:T(8,128)(2,1)S(1)} %collective-permute-done.36.gd0), channel_id=1, source_target_pairs={{0,1},{1,2},{2,3},{3,4},{4,5},{5,6},{6,7},{7,0},{8,9},{9,10},{10,1... | collective-permute-start | bytes 430088 | tf_op jit(solution)/shard_map/ppermute | solution.py:265
  347.2 14.7 %collective-permute-start.61 = (bf16[80,1792]{1,0:T(8,128)(2,1)S(1)}, bf16[80,1792]{1,0:T(8,128)(2,1)S(1)}, u32[]{:S(2)}, u32[]{:S(2)}) collective-permute-start(bf16[80,1792]{1,0:T(8,128)(2,1)S(1)} %fusion.9), channel_id=1, source_target_pairs={{0,1},{1,2},{2,3},{3,4},{4,5},{5,6},{6,7},{7,0},{8,9},{9,10},{10,1... | collective-permute-start | bytes 860168 | tf_op jit(solution)/shard_map/ppermute | solution.py:253
  357.0 40.2 %collective-permute-start.109 = (bf16[112,640]{1,0:T(8,128)(2,1)S(1)}, bf16[112,640]{1,0:T(8,128)(2,1)S(1)}, u32[]{:S(2)}, u32[]{:S(2)}) collective-permute-start(bf16[112,640]{1,0:T(8,128)(2,1)S(1)} %collective-permute-done.108.gd1), channel_id=1, source_target_pairs={{0,7},{1,0},{2,1},{3,2},{4,3},{5,4},{6,5},{7,6},{8,15},{9,8},{10,9... | collective-permute-start | bytes 430088 | tf_op jit(solution)/shard_map/ppermute | solution.py:265
  358.4 48.3 %collective-permute-start.95 = (bf16[112,640]{1,0:T(8,128)(2,1)}, bf16[112,640]{1,0:T(8,128)(2,1)S(1)}, u32[]{:S(2)}, u32[]{:S(2)}) collective-permute-start(bf16[112,640]{1,0:T(8,128)(2,1)} %collective-permute-done.94.gd0), channel_id=1, source_target_pairs={{0,1},{1,2},{2,3},{3,4},{4,5},{5,6},{6,7},{7,0},{8,9},{9,10},{10,1... | collective-permute-start | bytes 430088 | tf_op jit(solution)/shard_map/ppermute | solution.py:265
  360.2 46.8 %collective-permute-start.53 = (bf16[112,640]{1,0:T(8,128)(2,1)S(1)}, bf16[112,640]{1,0:T(8,128)(2,1)S(1)}, u32[]{:S(2)}, u32[]{:S(2)}) collective-permute-start(bf16[112,640]{1,0:T(8,128)(2,1)S(1)} %collective-permute-done.52.gd1), channel_id=1, source_target_pairs={{0,7},{1,0},{2,1},{3,2},{4,3},{5,4},{6,5},{7,6},{8,15},{9,8},{10,9... | collective-permute-start | bytes 430088 | tf_op jit(solution)/shard_map/ppermute | solution.py:265
  361.9 45.2 %collective-permute-start.39 = (bf16[112,640]{1,0:T(8,128)(2,1)S(1)}, bf16[112,640]{1,0:T(8,128)(2,1)S(1)}, u32[]{:S(2)}, u32[]{:S(2)}) collective-permute-start(bf16[112,640]{1,0:T(8,128)(2,1)S(1)} %collective-permute-done.38.gd0), channel_id=1, source_target_pairs={{0,1},{1,2},{2,3},{3,4},{4,5},{5,6},{6,7},{7,0},{8,9},{9,10},{10,1... | collective-permute-start | bytes 430088 | tf_op jit(solution)/shard_map/ppermute | solution.py:265
  407.1 15.1 %collective-permute-start.7 = (bf16[80,1792]{1,0:T(8,128)(2,1)S(1)}, bf16[80,1792]{1,0:T(8,128)(2,1)S(1)}, u32[]{:S(2)}, u32[]{:S(2)}) collective-permute-start(bf16[80,1792]{1,0:T(8,128)(2,1)S(1)} %fusion.21.gg), channel_id=1, source_target_pairs={{0,1},{1,2},{2,3},{3,4},{4,5},{5,6},{6,7},{7,0},{8,9},{9,10},{10,1... | collective-permute-start | bytes 860168 | tf_op jit(solution)/shard_map/ppermute | solution.py:265
  422.2 17.0 %collective-permute-start.65 = (bf16[80,1792]{1,0:T(8,128)(2,1)S(1)}, bf16[80,1792]{1,0:T(8,128)(2,1)S(1)}, u32[]{:S(2)}, u32[]{:S(2)}) collective-permute-start(bf16[80,1792]{1,0:T(8,128)(2,1)S(1)} %collective-permute-done.64.gg), channel_id=1, source_target_pairs={{0,1},{1,2},{2,3},{3,4},{4,5},{5,6},{6,7},{7,0},{8,9},{9,10},{10,1... | collective-permute-start | bytes 860168 | tf_op jit(solution)/shard_map/ppermute | solution.py:265
  432.7 15.9 %collective-permute-start.54 = (bf16[112,640]{1,0:T(8,128)(2,1)S(1)}, bf16[112,640]{1,0:T(8,128)(2,1)}, u32[]{:S(2)}, u32[]{:S(2)}) collective-permute-start(bf16[112,640]{1,0:T(8,128)(2,1)S(1)} %collective-permute-done.53.gd1), channel_id=1, source_target_pairs={{0,7},{1,0},{2,1},{3,2},{4,3},{5,4},{6,5},{7,6},{8,15},{9,8},{10,9... | collective-permute-start | bytes 430088 | tf_op jit(solution)/shard_map/ppermute | solution.py:265
  433.7 15.6 %collective-permute-start.23 = (bf16[80,1792]{1,0:T(8,128)(2,1)S(1)}, bf16[80,1792]{1,0:T(8,128)(2,1)S(1)}, u32[]{:S(2)}, u32[]{:S(2)}) collective-permute-start(bf16[80,1792]{1,0:T(8,128)(2,1)S(1)} %collective-permute-done.22.gu), channel_id=1, source_target_pairs={{0,7},{1,0},{2,1},{3,2},{4,3},{5,4},{6,5},{7,6},{8,15},{9,8},{10,9... | collective-permute-start | bytes 860168 | tf_op jit(solution)/shard_map/ppermute | solution.py:265
  434.5 17.5 %collective-permute-start.9 = (bf16[80,1792]{1,0:T(8,128)(2,1)S(1)}, bf16[80,1792]{1,0:T(8,128)(2,1)S(1)}, u32[]{:S(2)}, u32[]{:S(2)}) collective-permute-start(bf16[80,1792]{1,0:T(8,128)(2,1)S(1)} %collective-permute-done.8.gg), channel_id=1, source_target_pairs={{0,1},{1,2},{2,3},{3,4},{4,5},{5,6},{6,7},{7,0},{8,9},{9,10},{10,1... | collective-permute-start | bytes 860168 | tf_op jit(solution)/shard_map/ppermute | solution.py:265
  452.0 17.0 %collective-permute-start.67 = (bf16[80,1792]{1,0:T(8,128)(2,1)S(1)}, bf16[80,1792]{1,0:T(8,128)(2,1)S(1)}, u32[]{:S(2)}, u32[]{:S(2)}) collective-permute-start(bf16[80,1792]{1,0:T(8,128)(2,1)S(1)} %collective-permute-done.66.gg), channel_id=1, source_target_pairs={{0,1},{1,2},{2,3},{3,4},{4,5},{5,6},{6,7},{7,0},{8,9},{9,10},{10,1... | collective-permute-start | bytes 860168 | tf_op jit(solution)/shard_map/ppermute | solution.py:265
  453.2 15.8 %collective-permute-start.81 = (bf16[80,1792]{1,0:T(8,128)(2,1)S(1)}, bf16[80,1792]{1,0:T(8,128)(2,1)S(1)}, u32[]{:S(2)}, u32[]{:S(2)}) collective-permute-start(bf16[80,1792]{1,0:T(8,128)(2,1)S(1)} %collective-permute-done.80.gu), channel_id=1, source_target_pairs={{0,7},{1,0},{2,1},{3,2},{4,3},{5,4},{6,5},{7,6},{8,15},{9,8},{10,9... | collective-permute-start | bytes 860168 | tf_op jit(solution)/shard_map/ppermute | solution.py:265
  461.6 16.8 %collective-permute-start.111 = (bf16[112,640]{1,0:T(8,128)(2,1)S(1)}, bf16[112,640]{1,0:T(8,128)(2,1)S(1)}, u32[]{:S(2)}, u32[]{:S(2)}) collective-permute-start(bf16[112,640]{1,0:T(8,128)(2,1)S(1)} %copy-done.57), channel_id=1, source_target_pairs={{0,7},{1,0},{2,1},{3,2},{4,3},{5,4},{6,5},{7,6},{8,15},{9,8},{10,9... | collective-permute-start | bytes 430088 | tf_op jit(solution)/shard_map/ppermute | solution.py:265
  463.6 14.9 %collective-permute-start.25 = (bf16[80,1792]{1,0:T(8,128)(2,1)S(1)}, bf16[80,1792]{1,0:T(8,128)(2,1)S(1)}, u32[]{:S(2)}, u32[]{:S(2)}) collective-permute-start(bf16[80,1792]{1,0:T(8,128)(2,1)S(1)} %collective-permute-done.24.gu), channel_id=1, source_target_pairs={{0,7},{1,0},{2,1},{3,2},{4,3},{5,4},{6,5},{7,6},{8,15},{9,8},{10,9... | collective-permute-start | bytes 860168 | tf_op jit(solution)/shard_map/ppermute | solution.py:265
  464.3 17.4 %collective-permute-start.11 = (bf16[80,1792]{1,0:T(8,128)(2,1)S(1)}, bf16[80,1792]{1,0:T(8,128)(2,1)S(1)}, u32[]{:S(2)}, u32[]{:S(2)}) collective-permute-start(bf16[80,1792]{1,0:T(8,128)(2,1)S(1)} %collective-permute-done.10.gg), channel_id=1, source_target_pairs={{0,1},{1,2},{2,3},{3,4},{4,5},{5,6},{6,7},{7,0},{8,9},{9,10},{10,1... | collective-permute-start | bytes 860168 | tf_op jit(solution)/shard_map/ppermute | solution.py:265
  478.6 14.7 %collective-permute-start.26 = (bf16[80,1792]{1,0:T(8,128)(2,1)S(1)}, bf16[80,1792]{1,0:T(8,128)(2,1)}, u32[]{:S(2)}, u32[]{:S(2)}) collective-permute-start(bf16[80,1792]{1,0:T(8,128)(2,1)S(1)} %collective-permute-done.25.gu), channel_id=1, source_target_pairs={{0,7},{1,0},{2,1},{3,2},{4,3},{5,4},{6,5},{7,6},{8,15},{9,8},{10,9... | collective-permute-start | bytes 860168 | tf_op jit(solution)/shard_map/ppermute | solution.py:265
  481.8 14.7 %collective-permute-start.69 = (bf16[80,1792]{1,0:T(8,128)(2,1)S(1)}, bf16[80,1792]{1,0:T(8,128)(2,1)S(1)}, u32[]{:S(2)}, u32[]{:S(2)}) collective-permute-start(bf16[80,1792]{1,0:T(8,128)(2,1)S(1)} %collective-permute-done.68.gg), channel_id=1, source_target_pairs={{0,1},{1,2},{2,3},{3,4},{4,5},{5,6},{6,7},{7,0},{8,9},{9,10},{10,1... | collective-permute-start | bytes 860168 | tf_op jit(solution)/shard_map/ppermute | solution.py:265
  481.9 14.8 %collective-permute-start.83 = (bf16[80,1792]{1,0:T(8,128)(2,1)S(1)}, bf16[80,1792]{1,0:T(8,128)(2,1)S(1)}, u32[]{:S(2)}, u32[]{:S(2)}) collective-permute-start(bf16[80,1792]{1,0:T(8,128)(2,1)S(1)} %collective-permute-done.82.gu), channel_id=1, source_target_pairs={{0,7},{1,0},{2,1},{3,2},{4,3},{5,4},{6,5},{7,6},{8,15},{9,8},{10,9... | collective-permute-start | bytes 860168 | tf_op jit(solution)/shard_map/ppermute | solution.py:265
  491.3 55.4 %collective-permute-start.55 = (bf16[112,640]{1,0:T(8,128)(2,1)}, bf16[112,640]{1,0:T(8,128)(2,1)}, u32[]{:S(2)}, u32[]{:S(2)}) collective-permute-start(bf16[112,640]{1,0:T(8,128)(2,1)} %collective-permute-done.54.gd1), channel_id=1, source_target_pairs={{0,7},{1,0},{2,1},{3,2},{4,3},{5,4},{6,5},{7,6},{8,15},{9,8},{10,9... | collective-permute-start | bytes 430088 | tf_op jit(solution)/shard_map/ppermute | solution.py:265
  493.3 53.4 %collective-permute-start.41 = (bf16[112,640]{1,0:T(8,128)(2,1)}, bf16[112,640]{1,0:T(8,128)(2,1)}, u32[]{:S(2)}, u32[]{:S(2)}) collective-permute-start(bf16[112,640]{1,0:T(8,128)(2,1)} %collective-permute-done.40.gd0), channel_id=1, source_target_pairs={{0,1},{1,2},{2,3},{3,4},{4,5},{5,6},{6,7},{7,0},{8,9},{9,10},{10,1... | collective-permute-start | bytes 430088 | tf_op jit(solution)/shard_map/ppermute | solution.py:265
  493.4 53.3 %collective-permute-start.27 = (bf16[80,1792]{1,0:T(8,128)(2,1)}, bf16[80,1792]{1,0:T(8,128)(2,1)}, u32[]{:S(2)}, u32[]{:S(2)}) collective-permute-start(bf16[80,1792]{1,0:T(8,128)(2,1)} %collective-permute-done.26.gu), channel_id=1, source_target_pairs={{0,7},{1,0},{2,1},{3,2},{4,3},{5,4},{6,5},{7,6},{8,15},{9,8},{10,9... | collective-permute-start | bytes 860168 | tf_op jit(solution)/shard_map/ppermute | solution.py:265
  496.5 50.2 %collective-permute-start.13 = (bf16[80,1792]{1,0:T(8,128)(2,1)}, bf16[80,1792]{1,0:T(8,128)(2,1)}, u32[]{:S(2)}, u32[]{:S(2)}) collective-permute-start(bf16[80,1792]{1,0:T(8,128)(2,1)} %collective-permute-done.12.gg), channel_id=1, source_target_pairs={{0,1},{1,2},{2,3},{3,4},{4,5},{5,6},{6,7},{7,0},{8,9},{9,10},{10,1... | collective-permute-start | bytes 860168 | tf_op jit(solution)/shard_map/ppermute | solution.py:265
  (125 other events, 2341.3 us)

commit v2 on v1

v2 whole, which is shorter than its diff:
```python
import jax
import jax.numpy as jnp
from jax import lax
from jax.experimental import pallas as pl
from jax.experimental.pallas import tpu as pltpu
from jax.sharding import PartitionSpec as P


F32, BF16 = jnp.float32, jnp.bfloat16
COLS = 256
ROWS = 256
VMEM_LIMIT = 60 * 1024 * 1024


def dot(a, b, contract):
    return lax.dot_general(a, b, ((contract[:1], contract[1:]), ((), ())), preferred_element_type=F32)


def params(*semantics):
    return pltpu.CompilerParams(dimension_semantics=semantics, vmem_limit_bytes=VMEM_LIMIT)


def cost(flops, *arrays):
    return pl.CostEstimate(flops=flops, bytes_accessed=sum(a.size * a.dtype.itemsize for a in arrays), transcendentals=0)


def shaped(shape, dtype=BF16):
    return jax.ShapeDtypeStruct(shape, dtype)


def norm_scale(wide):
    return lax.rsqrt(jnp.mean(wide * wide, -1, keepdims=True) + 1e-6)


def forward_kernel(h_ref, wg_ref, wu_ref, wd_ref, next_ref, a_ref, act_ref):
    wide = h_ref[...].astype(F32)
    a = (wide * norm_scale(wide)).astype(BF16)
    a_ref[...] = a
    for j in range(act_ref.shape[1] // COLS):
        at = slice(j * COLS, (j + 1) * COLS)
        gate = dot(a, wg_ref[:, at], (1, 0))
        up = dot(a, wu_ref[:, at], (1, 0))
        act_ref[:, at] = (gate * jax.nn.sigmoid(gate) * up).astype(BF16)
    down = dot(act_ref[...], wd_ref[...], (1, 0)).astype(BF16).astype(F32)
    next_ref[...] = (h_ref[...].astype(F32) + down).astype(BF16)


def tiles_of(h, width):
    rows = min(h.shape[0], ROWS)
    return h.shape[0] // rows, pl.BlockSpec((rows, width), lambda i: (i, 0))


def matrix(w, number):
    return pl.BlockSpec((None, *w.shape[1:]), lambda i: (number, 0, 0))


def forward(h, wg, wu, wd, number):
    tokens, d = h.shape
    ff = wg.shape[2]
    grid, by_rows = tiles_of(h, d)
    _, hidden = tiles_of(h, ff)
    return pl.pallas_call(
        forward_kernel,
        grid=(grid,),
        in_specs=[by_rows] + [matrix(w, number) for w in (wg, wu, wd)],
        out_specs=[by_rows, by_rows, hidden],
        out_shape=[shaped((tokens, d)), shaped((tokens, d)), shaped((tokens, ff))],
        compiler_params=params("arbitrary"),
        cost_estimate=cost(6 * tokens * d * ff, h, h, h),
    )(h, wg, wu, wd)


def gate_kernel(h_ref, dy_ref, wg_ref, wu_ref, wd_ref, dg_ref, du_ref, a_ref, *act_ref):
    wide = h_ref[...].astype(F32)
    a = (wide * norm_scale(wide)).astype(BF16)
    a_ref[...] = a
    dy = dy_ref[...]
    for j in range(dg_ref.shape[1] // COLS):
        at = slice(j * COLS, (j + 1) * COLS)
        gate = dot(a, wg_ref[:, at], (1, 0))
        up = dot(a, wu_ref[:, at], (1, 0))
        by_act = dot(dy, wd_ref[at, :], (1, 1)).astype(BF16).astype(F32)
        s = jax.nn.sigmoid(gate)
        silu = gate * s
        if act_ref:
            act_ref[0][:, at] = (silu * up).astype(BF16)
        du_ref[:, at] = (by_act * silu).astype(BF16)
        dg_ref[:, at] = (by_act * up * (s + silu * (1.0 - s))).astype(BF16)


def gate_backward(h, dy, wg, wu, wd, number, with_act):
    tokens, d = h.shape
    ff = wg.shape[2]
    grid, by_rows = tiles_of(h, d)
    _, hidden = tiles_of(h, ff)
    extra = 1 if with_act else 0
    return pl.pallas_call(
        gate_kernel,
        grid=(grid,),
        in_specs=[by_rows, by_rows] + [matrix(w, number) for w in (wg, wu, wd)],
        out_specs=[hidden, hidden, by_rows] + [hidden] * extra,
        out_shape=[shaped((tokens, ff)), shaped((tokens, ff)), shaped((tokens, d))] + [shaped((tokens, ff))] * extra,
        compiler_params=params("arbitrary"),
        cost_estimate=cost(6 * tokens * d * ff, h, h, h),
    )(h, dy, wg, wu, wd)


def states_kernel(h_ref, dy_ref, dg_ref, du_ref, wg_ref, wu_ref, out_ref):
    by_a = dot(dg_ref[...], wg_ref[...], (1, 1)) + dot(du_ref[...], wu_ref[...], (1, 1))
    by_a = by_a.astype(BF16).astype(F32)
    wide = h_ref[...].astype(F32)
    scale = norm_scale(wide)
    along = jnp.mean(by_a * wide, -1, keepdims=True)
    by_h = (by_a * scale - wide * (scale * scale * scale * along)).astype(BF16)
    out_ref[...] = (dy_ref[...].astype(F32) + by_h.astype(F32)).astype(BF16)


def states_backward(h, dy, dg, du, wg, wu, number):
    tokens, d = h.shape
    ff = wg.shape[2]
    grid, by_rows = tiles_of(h, d)
    _, hidden = tiles_of(h, ff)
    return pl.pallas_call(
        states_kernel,
        grid=(grid,),
        in_specs=[by_rows, by_rows, hidden, hidden, matrix(wg, number), matrix(wu, number)],
        out_specs=by_rows,
        out_shape=shaped((tokens, d)),
        compiler_params=params("arbitrary"),
        cost_estimate=cost(4 * tokens * d * ff, h, h, h),
    )(h, dy, dg, du, wg, wu)


def weight_gradient(a, b):
    a, b = lax.optimization_barrier((a, b))
    return lax.optimization_barrier(dot(a, b, (0, 0)).astype(BF16))


def adamw(w_ref, m_ref, v_ref, g_ref, w_out, m_out, v_out):
    g = g_ref[...].astype(F32)
    m = 0.9 * m_ref[...] + 0.1 * g
    v = 0.95 * v_ref[...] + 0.05 * g * g
    step = m * lax.rsqrt(v + 1e-8) + 0.1 * w_ref[...].astype(F32)
    w_out[...] = (w_ref[...].astype(F32) - 0.02 * step).astype(BF16)
    m_out[...] = m
    v_out[...] = v


def adamw_kernel(ids_ref, gg, gu, gd0, gd1, *refs):
    ins, outs = refs[:9], refs[-9:]
    way = pl.program_id(0)

    def one(which, g_ref):
        adamw(ins[which], ins[3 + which], ins[6 + which], g_ref, outs[which], outs[3 + which], outs[6 + which])

    @pl.when(way == 0)
    def _():
        one(0, gg)
        one(2, gd0)

    @pl.when(way == 1)
    def _():
        one(1, gu)
        one(2, gd1)


def adamw_step(ids, pieces, arrays, so_far, number):
    gg, gu, gd0, _ = pieces
    whole = lambda g: pl.BlockSpec(g.shape, lambda way, ids: (0, 0))
    gate = pl.BlockSpec((None, *gg.shape), lambda way, ids: (number, ids[0], 0))
    up = pl.BlockSpec((None, *gu.shape), lambda way, ids: (number, ids[1], 0))
    down = pl.BlockSpec((None, *gd0.shape), lambda way, ids: (number, 2 * ids[way] + way, 0))
    nine = [gate, up, down] * 3
    in_specs = [whole(g) for g in pieces] + nine
    aliases = {}
    operands = [*pieces, *arrays]
    if so_far is not None:
        in_specs += [pl.BlockSpec(memory_space=pl.ANY)] * 9
        aliases = {1 + len(operands) + i: i for i in range(9)}
        operands += so_far
    return pl.pallas_call(
        adamw_kernel,
        grid_spec=pltpu.PrefetchScalarGridSpec(num_scalar_prefetch=1, grid=(2,), in_specs=in_specs, out_specs=nine),
        out_shape=[shaped(a.shape, a.dtype) for a in arrays],
        input_output_aliases=aliases,
        compiler_params=params("arbitrary"),
        cost_estimate=pl.CostEstimate(flops=4_000_000_000, bytes_accessed=22 * sum(g.size for g in pieces), transcendentals=0),
    )(ids, *operands)


class Reduce:
    def __init__(self, me, n, ways, local, way, parts, part):
        self.me, self.n, self.way, self.pairs = me, n, way, ways[way]
        self.parts, self.part, self.left = parts, part, n - 1
        self.slabs = local.reshape(n * parts, local.shape[0] // (n * parts), local.shape[1])
        self.value = self.own()

    def own(self):
        at = self.n - self.left
        chunk = lax.rem(self.me + 2 * self.n + (-at if self.way == 0 else at), self.n)
        return lax.dynamic_index_in_dim(self.slabs, chunk * self.parts + self.part, 0, False)

    def send(self):
        self.come = lax.ppermute(self.value, "dp", self.pairs)

    def receive(self):
        self.left -= 1
        self.value = (self.come.astype(F32) + self.own().astype(F32)).astype(BF16)


class Gather:
    def __init__(self, value, pairs):
        self.value, self.pairs = value, pairs

    def send(self):
        self.come = lax.ppermute(self.value, "dp", self.pairs)

    def receive(self):
        self.value = self.come


def solution(mesh):
    n = mesh.shape["dp"]
    ways = ([(i, (i + 1) % n) for i in range(n)], [(i, (i - 1) % n) for i in range(n)])

    def step(x, dy, *arrays):
        wg, wu, wd = arrays[:3]
        me = lax.axis_index("dp")

        def slot(rings, kernel):
            for ring in rings:
                ring.send()
            out = kernel()
            for ring in rings:
                ring.receive()
            if rings:
                for ring, value in zip(rings, lax.optimization_barrier([ring.value for ring in rings]), strict=True):
                    ring.value = value
            return out

        def reduce(local, way, parts=1, part=0):
            return Reduce(me, n, ways, local, way, parts, part)

        def both(down):
            return [reduce(down, way, 2, way) for way in (0, 1)]

        def layer(gate, up, down):
            return [reduce(gate, 0), reduce(up, 1), *both(down)]

        h0, by_y = x[0], dy[0]
        h1, a0, act0 = forward(h0, wg, wu, wd, 0)
        dg1, du1, a1, act1 = gate_backward(h1, by_y, wg, wu, wd, 1, True)
        rings = {1: layer(weight_gradient(a1, dg1), weight_gradient(a1, du1), weight_gradient(act1, by_y))}
        by_h = slot(rings[1], lambda: states_backward(h1, by_y, dg1, du1, wg, wu, 1))
        dg0, du0, _ = slot(rings[1], lambda: gate_backward(h0, by_h, wg, wu, wd, 0, False))
        rings[0] = layer(weight_gradient(a0, dg0), weight_gradient(a0, du0), weight_gradient(act0, by_h))
        so_far, brought = None, {1: None, 0: None}

        def advance(number):
            nonlocal so_far
            if brought[number] is None:
                slot(rings[number], lambda: None)
                if rings[number][0].left == 0:
                    rings[number] = [Gather(r.value, r.pairs) for r in rings[number]]
                    brought[number] = 0
                return
            s = brought[number]
            brought[number] += 1
            ids = jnp.stack([lax.rem(me + n - s, n), lax.rem(me + s, n)])
            pieces = [ring.value for ring in rings[number]]
            going = rings[number] if s < n - 1 else []
            so_far = slot(going, lambda: list(adamw_step(ids, pieces, arrays, so_far, number)))

        while brought[0] != n:
            for number in (1, 0):
                if brought[number] != n:
                    advance(number)
        return tuple(so_far)

    step = jax.shard_map(
        step,
        mesh=mesh,
        in_specs=(P(("rep", "dp"), None, None),) * 2 + (P(None, None, None),) * 9,
        out_specs=(P("rep", None, None),) * 9,
        check_vma=False,
    )
    return step
```

time: 562 us -> 491 us (0.87)
  Pallas kernels: 268 us -> 190 us
  matrix products: 0 us -> 50.7 us
  waiting for transfers between devices: 92.3 us -> 52.2 us
  starting transfers between devices: 161 us -> 167 us
  other arithmetic: 20.2 us -> 14.5 us
    pallas_call x12 -> x4, Pallas kernels: 170 us -> 91.6 us  [the longest x2 49.9 us: gate_backward(): pl.pallas_call(gate_kernel, grid=(grid,), in_specs=[by_rows, by_rows] + [...]
    dot_general x0 -> x6, matrix products: none -> 50.7 us  [dot(): lax.dot_general(a, b, ((contract[:1], contract[1:]), ((), ())), preferred...]
    ppermute x112, waiting for transfers between devices: 92.3 us -> 52.2 us  [send(): self.come = lax.ppermute(self.value, 'dp', self.pairs)]
    ppermute x112, starting transfers between devices: 161 us -> 167 us  [send(): self.come = lax.ppermute(self.value, 'dp', self.pairs)]
  transfers between devices with their start and end apart: 112 -> 112, of which waited for: 36 -> 26; matrix products, arithmetic and copies ran while one was open for 5% -> 13% of each run, Pallas kernels for 35% -> 24%
where the time goes in v2:
time: 491 us; the launch traced here: 484 us
  Pallas kernels  190 us (39%)
  starting transfers between devices  167 us (34%)
  waiting for transfers between devices  52.2 us (11%)
  matrix products  50.7 us (10%)
  other arithmetic  14.5 us (3%)
  local copies, waits for them, and re-layouts  6.85 us (1%)
    ppermute x112, starting transfers between devices, send(): self.come = lax.ppermute(self.value, 'dp', self.pairs)  167 us
    pallas_call x16, Pallas kernels, adamw_step(): pl.pallas_call(adamw_kernel, grid_spec=pltpu.PrefetchScalarGridSpec(num_s...  98.2 us
    ppermute x112, waiting for transfers between devices, send(): self.come = lax.ppermute(self.value, 'dp', self.pairs)  52.2 us
    dot_general x6, matrix products, dot(): lax.dot_general(a, b, ((contract[:1], contract[1:]), ((), ())), preferred...  50.7 us
    pallas_call x2, Pallas kernels, gate_backward(): pl.pallas_call(gate_kernel, grid=(grid,), in_specs=[by_rows, by_rows] + [...  49.9 us
    pallas_call x1, Pallas kernels, forward(): pl.pallas_call(forward_kernel, grid=(grid,), in_specs=[by_rows] + [matrix...  23.3 us
    pallas_call x1, Pallas kernels, states_backward(): pl.pallas_call(states_kernel, grid=(grid,), in_specs=[by_rows, by_rows, h...  18.4 us
    convert_element_type x42, other arithmetic, receive(): self.value = (self.come.astype(F32) + self.own().astype(F32)).astype(BF16)  11.3 us
  transfers between devices with their start and end apart: 112, of which 26 were waited for; matrix products, arithmetic and copies ran while one was open for 13% of the time, Pallas kernels for 24%

profile of v2, /device:TPU:30, one launch (start us, length us, event | category | flops | bytes accessed | tf_op | source)
XLA Modules:
  0.0 483.9 jit_solution(5694701421004386347)
XLA Ops:
  0.7 23.3 %shard_map.178 = (bf16[2048,640]{1,0:T(8,128)(2,1)}, bf16[2048,640]{1,0:T(8,128)(2,1)}, bf16[2048,1792]{1,0:T(8,128)(2,1)}) custom-call(bf16[2048,640]{1,0:T(8,128)(2,1)} %bitcast.264, bf16[2,640,1792]{2,1,0:T(8,128)(2,1)} %refs_0_.31, bf16[2,640,1792]{2,1,0:T(8,128)(2,1)} %refs_1_.31, bf16[2,1792,640]{2,1,0:T(8,128)(2,1)} %refs_2_.31), custom_call_target="tpu_custom_call" | custom-call | flops 14092861440 | bytes 7864320 | tf_op jit(solution)/shard_map/pallas_call | solution.py:62
  24.0 24.9 %shard_map.179 = (bf16[2048,1792]{1,0:T(8,128)(2,1)}, bf16[2048,1792]{1,0:T(8,128)(2,1)}, bf16[2048,640]{1,0:T(8,128)(2,1)}, bf16[2048,1792]{1,0:T(8,128)(2,1)}) custom-call(bf16[2048,640]{1,0:T(8,128)(2,1)} %get-tuple-element.278.h_ref, bf16[2048,640]{1,0:T(8,128)(2,1)} %bitcast.261, bf16[2,640,1792]{2,1,0:T(8,128)(2,1)} %refs_0_.31, ...), custom_call_target="tpu_custom_call" | custom-call | flops 14092861440 | bytes 7864320 | tf_op jit(solution)/shard_map/pallas_call | solution.py:97
  48.9 9.0 %convolution_convert_fusion = bf16[1792,640]{1,0:T(8,128)(2,1)S(1)} fusion(bf16[2048,1792]{1,0:T(8,128)(2,1)} %get-tuple-element.352, bf16[2048,640]{1,0:T(8,128)(2,1)} %bitcast.262), kind=kOutput, calls=%fused_computation | convolution fusion | flops 4698767360 | bytes 12255232 | tf_op jit(solution)/shard_map/dot_general | solution.py:16
  58.8 7.3 %collective-permute-start.59 = (bf16[112,640]{1,0:T(8,128)(2,1)}, bf16[112,640]{1,0:T(8,128)(2,1)}, u32[]{:S(2)}, u32[]{:S(2)}) collective-permute-start(bf16[112,640]{1,0:T(8,128)(2,1)} %get-tuple-element.559), channel_id=1, source_target_pairs={{0,7},{1,0},{2,1},{3,2},{4,3},{5,4},{6,5},{7,6},{8,15},{9,8},{10,9... | collective-permute-start | bytes 430088 | tf_op jit(solution)/shard_map/ppermute | solution.py:204
  66.2 18.4 %shard_map.180.dy_ref = bf16[2048,640]{1,0:T(8,128)(2,1)} custom-call(bf16[2048,640]{1,0:T(8,128)(2,1)} %get-tuple-element.278.h_ref, bf16[2048,640]{1,0:T(8,128)(2,1)} %bitcast.263, bf16[2048,1792]{1,0:T(8,128)(2,1)} %get-tuple-element.348.dg_ref, bf16[2048,1792]{1,0:T(8,128)(2,1)} %get-tuple-element.350.du_ref, bf16[2,640,1792]{2,1,0:T(8,128)(2,1)} %refs_0_.31, ...), custom_call_target="tpu_custom_call" | custom-call | flops 9395240960 | bytes 7864320 | tf_op jit(solution)/shard_map/pallas_call | solution.py:123
  84.7 9.0 %convolution_convert_fusion.3 = bf16[1792,640]{1,0:T(8,128)(2,1)S(1)} fusion(bf16[2048,1792]{1,0:T(8,128)(2,1)} %get-tuple-element.288, bf16[2048,640]{1,0:T(8,128)(2,1)} %shard_map.180.dy_ref), kind=kOutput, calls=%fused_computation.3 | convolution fusion | flops 4698767360 | bytes 12255232 | tf_op jit(solution)/shard_map/dot_general | solution.py:16
  97.7 8.9 %convolution_convert_fusion.2 = bf16[640,1792]{1,0:T(8,128)(2,1)S(1)} fusion(bf16[2048,640]{1,0:T(8,128)(2,1)} %get-tuple-element.349, bf16[2048,1792]{1,0:T(8,128)(2,1)} %get-tuple-element.348.dg_ref), kind=kOutput, calls=%fused_computation.2 | convolution fusion | flops 4698767360 | bytes 12255232 | tf_op jit(solution)/shard_map/dot_general | solution.py:16
  106.7 24.9 %shard_map.181 = (bf16[2048,1792]{1,0:T(8,128)(2,1)}, bf16[2048,1792]{1,0:T(8,128)(2,1)}, bf16[2048,640]{1,0:T(8,128)(2,1)}) custom-call(bf16[2048,640]{1,0:T(8,128)(2,1)} %bitcast.265, bf16[2048,640]{1,0:T(8,128)(2,1)} %shard_map.180.dy_ref, bf16[2,640,1792]{2,1,0:T(8,128)(2,1)} %refs_0_.31, bf16[2,640,1792]{2,1,0:T(8,128)(2,1)} %refs_1_.31, ...), custom_call_target="tpu_custom_call" | custom-call | flops 14092861440 | bytes 7864320 | tf_op jit(solution)/shard_map/pallas_call | solution.py:97
  131.7 10.4 %convolution_convert_fusion.1 = bf16[640,1792]{1,0:T(8,128)(2,1)} fusion(bf16[2048,640]{1,0:T(8,128)(2,1)} %get-tuple-element.349, bf16[2048,1792]{1,0:T(8,128)(2,1)} %get-tuple-element.350.du_ref), kind=kOutput, calls=%fused_computation.1 | convolution fusion | flops 4698767360 | bytes 12255232 | tf_op jit(solution)/shard_map/dot_general | solution.py:16
  142.1 6.6 %convolution_convert_fusion.5 = bf16[640,1792]{1,0:T(8,128)(2,1)} fusion(bf16[2048,640]{1,0:T(8,128)(2,1)S(1)} %copy-done.74, bf16[2048,1792]{1,0:T(8,128)(2,1)S(1)} %copy-done.73), kind=kOutput, calls=%fused_computation.5 | convolution fusion | flops 4698767360 | bytes 12255232 | tf_op jit(solution)/shard_map/dot_general | solution.py:16
  148.7 6.8 %convolution_convert_fusion.4 = bf16[640,1792]{1,0:T(8,128)(2,1)} fusion(bf16[2048,640]{1,0:T(8,128)(2,1)S(1)} %copy-done.74, bf16[2048,1792]{1,0:T(8,128)(2,1)S(1)} %bitcast.267), kind=kOutput, calls=%fused_computation.4 | convolution fusion | flops 4698767360 | bytes 12255232 | tf_op jit(solution)/shard_map/dot_general | solution.py:16
  165.6 3.3 collective-permute-start.1
  173.1 3.7 collective-permute-start.63
  186.5 3.6 collective-permute-done.6
  203.3 5.3 %collective-permute-done.10 = bf16[112,640]{1,0:T(8,128)(2,1)S(1)} collective-permute-done((bf16[112,640]{1,0:T(8,128)(2,1)S(1)}, bf16[112,640]{1,0:T(8,128)(2,1)S(1)}, u32[]{:S(2)}, u32[]{:S(2)}) %collective-permute-start.10) | collective-permute-done | bytes 143392 | tf_op jit(solution)/shard_map/ppermute | solution.py:204
  222.1 5.9 %collective-permute-done.14 = bf16[112,640]{1,0:T(8,128)(2,1)S(1)} collective-permute-done((bf16[112,640]{1,0:T(8,128)(2,1)S(1)}, bf16[112,640]{1,0:T(8,128)(2,1)S(1)}, u32[]{:S(2)}, u32[]{:S(2)}) %collective-permute-start.14) | collective-permute-done | bytes 143392 | tf_op jit(solution)/shard_map/ppermute | solution.py:204
  241.2 5.4 %collective-permute-done.18 = bf16[112,640]{1,0:T(8,128)(2,1)S(1)} collective-permute-done((bf16[112,640]{1,0:T(8,128)(2,1)S(1)}, bf16[112,640]{1,0:T(8,128)(2,1)S(1)}, u32[]{:S(2)}, u32[]{:S(2)}) %collective-permute-start.18) | collective-permute-done | bytes 143392 | tf_op jit(solution)/shard_map/ppermute | solution.py:204
  259.8 5.4 %collective-permute-done.22 = bf16[112,640]{1,0:T(8,128)(2,1)S(1)} collective-permute-done((bf16[112,640]{1,0:T(8,128)(2,1)S(1)}, bf16[112,640]{1,0:T(8,128)(2,1)S(1)}, u32[]{:S(2)}, u32[]{:S(2)}) %collective-permute-start.22) | collective-permute-done | bytes 143392 | tf_op jit(solution)/shard_map/ppermute | solution.py:204
  278.4 5.3 %collective-permute-done.26 = bf16[112,640]{1,0:T(8,128)(2,1)S(1)} collective-permute-done((bf16[112,640]{1,0:T(8,128)(2,1)S(1)}, bf16[112,640]{1,0:T(8,128)(2,1)S(1)}, u32[]{:S(2)}, u32[]{:S(2)}) %collective-permute-start.26) | collective-permute-done | bytes 143392 | tf_op jit(solution)/shard_map/ppermute | solution.py:204
  305.8 6.1 %shard_map.182 = (bf16[2,640,1792]{2,1,0:T(8,128)(2,1)}, bf16[2,640,1792]{2,1,0:T(8,128)(2,1)}, bf16[2,1792,640]{2,1,0:T(8,128)(2,1)}, f32[2,640,1792]{2,1,0:T(8...) custom-call(s32[2]{0:T(128)} %pad_add_fusion.7.ids_ref, ...), custom_call_target="tpu_custom_call" | custom-call | flops 4000000000 | bytes 9461760 | tf_op jit(solution)/shard_map/pallas_call | solution.py:181
  312.0 3.3 collective-permute-start.89
  315.5 3.3 collective-permute-start.35
  322.6 6.2 %shard_map.183 = (bf16[2,640,1792]{2,1,0:T(8,128)(2,1)}, bf16[2,640,1792]{2,1,0:T(8,128)(2,1)}, bf16[2,1792,640]{2,1,0:T(8,128)(2,1)}, f32[2,640,1792]{2,1,0:T(8...) custom-call(s32[2]{0:T(128)} %get-tuple-element.582.ids_ref, ...), custom_call_target="tpu_custom_call", output_to_operand_aliasing={{0}: (14, {}), {1}: (15, {}), {2}: (16, {}), {3}: (17, {}),... | custom-call | flops 4000000000 | bytes 9461760 | tf_op jit(solution)/shard_map/pallas_call | solution.py:181
  329.0 3.3 collective-permute-start.95
  335.6 6.2 %shard_map.184 = (bf16[2,640,1792]{2,1,0:T(8,128)(2,1)}, bf16[2,640,1792]{2,1,0:T(8,128)(2,1)}, bf16[2,1792,640]{2,1,0:T(8,128)(2,1)}, f32[2,640,1792]{2,1,0:T(8...) custom-call(s32[2]{0:T(128)} %get-tuple-element.581.ids_ref, ...), custom_call_target="tpu_custom_call", output_to_operand_aliasing={{0}: (14, {}), {1}: (15, {}), {2}: (16, {}), {3}: (17, {}),... | custom-call | flops 4000000000 | bytes 9461760 | tf_op jit(solution)/shard_map/pallas_call | solution.py:181
  341.8 3.3 collective-permute-start.39
  345.2 3.3 collective-permute-start.37
  348.5 6.1 %shard_map.185 = (bf16[2,640,1792]{2,1,0:T(8,128)(2,1)}, bf16[2,640,1792]{2,1,0:T(8,128)(2,1)}, bf16[2,1792,640]{2,1,0:T(8,128)(2,1)}, f32[2,640,1792]{2,1,0:T(8...) custom-call(s32[2]{0:T(128)} %pad_add_fusion.7.ids_ref, ...), custom_call_target="tpu_custom_call", output_to_operand_aliasing={{0}: (14, {}), {1}: (15, {}), {2}: (16, {}), {3}: (17, {}),... | custom-call | flops 4000000000 | bytes 9461760 | tf_op jit(solution)/shard_map/pallas_call | solution.py:181
  354.8 3.3 collective-permute-start.99
  361.4 6.2 %shard_map.186 = (bf16[2,640,1792]{2,1,0:T(8,128)(2,1)}, bf16[2,640,1792]{2,1,0:T(8,128)(2,1)}, bf16[2,1792,640]{2,1,0:T(8,128)(2,1)}, f32[2,640,1792]{2,1,0:T(8...) custom-call(s32[2]{0:T(128)} %get-tuple-element.580.ids_ref, ...), custom_call_target="tpu_custom_call", output_to_operand_aliasing={{0}: (14, {}), {1}: (15, {}), {2}: (16, {}), {3}: (17, {}),... | custom-call | flops 4000000000 | bytes 9461760 | tf_op jit(solution)/shard_map/pallas_call | solution.py:181
  371.1 3.3 collective-permute-start.41
  374.3 6.1 %shard_map.187 = (bf16[2,640,1792]{2,1,0:T(8,128)(2,1)}, bf16[2,640,1792]{2,1,0:T(8,128)(2,1)}, bf16[2,1792,640]{2,1,0:T(8,128)(2,1)}, f32[2,640,1792]{2,1,0:T(8...) custom-call(s32[2]{0:T(128)} %get-tuple-element.582.ids_ref, ...), custom_call_target="tpu_custom_call", output_to_operand_aliasing={{0}: (14, {}), {1}: (15, {}), {2}: (16, {}), {3}: (17, {}),... | custom-call | flops 4000000000 | bytes 9461760 | tf_op jit(solution)/shard_map/pallas_call | solution.py:181
  380.6 3.3 collective-permute-start.103
  387.5 6.2 %shard_map.188 = (bf16[2,640,1792]{2,1,0:T(8,128)(2,1)}, bf16[2,640,1792]{2,1,0:T(8,128)(2,1)}, bf16[2,1792,640]{2,1,0:T(8,128)(2,1)}, f32[2,640,1792]{2,1,0:T(8...) custom-call(s32[2]{0:T(128)} %get-tuple-element.579.ids_ref, ...), custom_call_target="tpu_custom_call", output_to_operand_aliasing={{0}: (14, {}), {1}: (15, {}), {2}: (16, {}), {3}: (17, {}),... | custom-call | flops 4000000000 | bytes 9461760 | tf_op jit(solution)/shard_map/pallas_call | solution.py:181
  397.0 3.3 collective-permute-start.45
  400.3 6.1 %shard_map.189 = (bf16[2,640,1792]{2,1,0:T(8,128)(2,1)}, bf16[2,640,1792]{2,1,0:T(8,128)(2,1)}, bf16[2,1792,640]{2,1,0:T(8,128)(2,1)}, f32[2,640,1792]{2,1,0:T(8...) custom-call(s32[2]{0:T(128)} %get-tuple-element.581.ids_ref, ...), custom_call_target="tpu_custom_call", output_to_operand_aliasing={{0}: (14, {}), {1}: (15, {}), {2}: (16, {}), {3}: (17, {}),... | custom-call | flops 4000000000 | bytes 9461760 | tf_op jit(solution)/shard_map/pallas_call | solution.py:181
  406.6 3.3 collective-permute-start.107
  413.2 6.2 %shard_map.190 = (bf16[2,640,1792]{2,1,0:T(8,128)(2,1)}, bf16[2,640,1792]{2,1,0:T(8,128)(2,1)}, bf16[2,1792,640]{2,1,0:T(8,128)(2,1)}, f32[2,640,1792]{2,1,0:T(8...) custom-call(s32[2]{0:T(128)} %get-tuple-element.578.ids_ref, ...), custom_call_target="tpu_custom_call", output_to_operand_aliasing={{0}: (14, {}), {1}: (15, {}), {2}: (16, {}), {3}: (17, {}),... | custom-call | flops 4000000000 | bytes 9461760 | tf_op jit(solution)/shard_map/pallas_call | solution.py:181
  422.9 3.3 collective-permute-start.49
  426.1 6.1 %shard_map.191 = (bf16[2,640,1792]{2,1,0:T(8,128)(2,1)}, bf16[2,640,1792]{2,1,0:T(8,128)(2,1)}, bf16[2,1792,640]{2,1,0:T(8,128)(2,1)}, f32[2,640,1792]{2,1,0:T(8...) custom-call(s32[2]{0:T(128)} %get-tuple-element.580.ids_ref, ...), custom_call_target="tpu_custom_call", output_to_operand_aliasing={{0}: (14, {}), {1}: (15, {}), {2}: (16, {}), {3}: (17, {}),... | custom-call | flops 4000000000 | bytes 9461760 | tf_op jit(solution)/shard_map/pallas_call | solution.py:181
  432.4 3.3 collective-permute-start.111
  439.1 6.2 %shard_map.192 = (bf16[2,640,1792]{2,1,0:T(8,128)(2,1)}, bf16[2,640,1792]{2,1,0:T(8,128)(2,1)}, bf16[2,1792,640]{2,1,0:T(8,128)(2,1)}, f32[2,640,1792]{2,1,0:T(8...) custom-call(s32[2]{0:T(128)} %get-tuple-element.577.ids_ref, ...), custom_call_target="tpu_custom_call", output_to_operand_aliasing={{0}: (14, {}), {1}: (15, {}), {2}: (16, {}), {3}: (17, {}),... | custom-call | flops 4000000000 | bytes 9461760 | tf_op jit(solution)/shard_map/pallas_call | solution.py:181
  448.7 3.5 collective-permute-start.53
  452.2 6.1 %shard_map.193 = (bf16[2,640,1792]{2,1,0:T(8,128)(2,1)}, bf16[2,640,1792]{2,1,0:T(8,128)(2,1)}, bf16[2,1792,640]{2,1,0:T(8,128)(2,1)}, f32[2,640,1792]{2,1,0:T(8...) custom-call(s32[2]{0:T(128)} %get-tuple-element.579.ids_ref, ...), custom_call_target="tpu_custom_call", output_to_operand_aliasing={{0}: (14, {}), {1}: (15, {}), {2}: (16, {}), {3}: (17, {}),... | custom-call | flops 4000000000 | bytes 9461760 | tf_op jit(solution)/shard_map/pallas_call | solution.py:181
  459.0 6.1 %shard_map.194 = (bf16[2,640,1792]{2,1,0:T(8,128)(2,1)}, bf16[2,640,1792]{2,1,0:T(8,128)(2,1)}, bf16[2,1792,640]{2,1,0:T(8,128)(2,1)}, f32[2,640,1792]{2,1,0:T(8...) custom-call(s32[2]{0:T(128)} %pad_add_fusion.ids_ref, ...), custom_call_target="tpu_custom_call", output_to_operand_aliasing={{0}: (14, {}), {1}: (15, {}), {2}: (16, {}), {3}: (17, {}),... | custom-call | flops 4000000000 | bytes 9461760 | tf_op jit(solution)/shard_map/pallas_call | solution.py:181
  465.2 6.2 %shard_map.195 = (bf16[2,640,1792]{2,1,0:T(8,128)(2,1)}, bf16[2,640,1792]{2,1,0:T(8,128)(2,1)}, bf16[2,1792,640]{2,1,0:T(8,128)(2,1)}, f32[2,640,1792]{2,1,0:T(8...) custom-call(s32[2]{0:T(128)} %get-tuple-element.578.ids_ref, ...), custom_call_target="tpu_custom_call", output_to_operand_aliasing={{0}: (14, {}), {1}: (15, {}), {2}: (16, {}), {3}: (17, {}),... | custom-call | flops 4000000000 | bytes 9461760 | tf_op jit(solution)/shard_map/pallas_call | solution.py:181
  471.3 6.2 %shard_map.196 = (bf16[2,640,1792]{2,1,0:T(8,128)(2,1)}, bf16[2,640,1792]{2,1,0:T(8,128)(2,1)}, bf16[2,1792,640]{2,1,0:T(8,128)(2,1)}, f32[2,640,1792]{2,1,0:T(8...) custom-call(s32[2]{0:T(128)} %get-tuple-element.577.ids_ref, ...), custom_call_target="tpu_custom_call", output_to_operand_aliasing={{0}: (14, {}), {1}: (15, {}), {2}: (16, {}), {3}: (17, {}),... | custom-call | flops 4000000000 | bytes 9461760 | tf_op jit(solution)/shard_map/pallas_call | solution.py:181
  477.5 6.2 %shard_map.197 = (bf16[2,640,1792]{2,1,0:T(8,128)(2,1)}, bf16[2,640,1792]{2,1,0:T(8,128)(2,1)}, bf16[2,1792,640]{2,1,0:T(8,128)(2,1)}, f32[2,640,1792]{2,1,0:T(8...) custom-call(s32[2]{0:T(128)} %pad_add_fusion.ids_ref, ...), custom_call_target="tpu_custom_call", output_to_operand_aliasing={{0}: (14, {}), {1}: (15, {}), {2}: (16, {}), {3}: (17, {}),... | custom-call | flops 4000000000 | bytes 9461760 | tf_op jit(solution)/shard_map/pallas_call | solution.py:181
  (410 shorter events, 152.5 us)
Async XLA Ops:
  58.8 102.4 %collective-permute-start.59 = (bf16[112,640]{1,0:T(8,128)(2,1)}, bf16[112,640]{1,0:T(8,128)(2,1)}, u32[]{:S(2)}, u32[]{:S(2)}) collective-permute-start(bf16[112,640]{1,0:T(8,128)(2,1)} %get-tuple-element.559), channel_id=1, source_target_pairs={{0,7},{1,0},{2,1},{3,2},{4,3},{5,4},{6,5},{7,6},{8,15},{9,8},{10,9... | collective-permute-start | bytes 430088 | tf_op jit(solution)/shard_map/ppermute | solution.py:204
  66.0 98.4 %collective-permute-start.58 = (bf16[112,640]{1,0:T(8,128)(2,1)}, bf16[112,640]{1,0:T(8,128)(2,1)}, u32[]{:S(2)}, u32[]{:S(2)}) collective-permute-start(bf16[112,640]{1,0:T(8,128)(2,1)} %get-tuple-element.560), channel_id=1, source_target_pairs={{0,1},{1,2},{2,3},{3,4},{4,5},{5,6},{6,7},{7,0},{8,9},{9,10},{10,1... | collective-permute-start | bytes 430088 | tf_op jit(solution)/shard_map/ppermute | solution.py:204
  94.5 71.1 %collective-permute-start.3 = (bf16[112,640]{1,0:T(8,128)(2,1)}, bf16[112,640]{1,0:T(8,128)(2,1)}, u32[]{:S(2)}, u32[]{:S(2)}) collective-permute-start(bf16[112,640]{1,0:T(8,128)(2,1)} %get-tuple-element.575), channel_id=1, source_target_pairs={{0,7},{1,0},{2,1},{3,2},{4,3},{5,4},{6,5},{7,6},{8,15},{9,8},{10,9... | collective-permute-start | bytes 430088 | tf_op jit(solution)/shard_map/ppermute | solution.py:204
  97.7 71.3 %collective-permute-start.2 = (bf16[112,640]{1,0:T(8,128)(2,1)}, bf16[112,640]{1,0:T(8,128)(2,1)}, u32[]{:S(2)}, u32[]{:S(2)}) collective-permute-start(bf16[112,640]{1,0:T(8,128)(2,1)} %get-tuple-element.576), channel_id=1, source_target_pairs={{0,1},{1,2},{2,3},{3,4},{4,5},{5,6},{6,7},{7,0},{8,9},{9,10},{10,1... | collective-permute-start | bytes 430088 | tf_op jit(solution)/shard_map/ppermute | solution.py:204
  106.6 63.6 %collective-permute-start.56 = (bf16[80,1792]{1,0:T(8,128)(2,1)S(1)}, bf16[80,1792]{1,0:T(8,128)(2,1)S(1)}, u32[]{:S(2)}, u32[]{:S(2)}) collective-permute-start(bf16[80,1792]{1,0:T(8,128)(2,1)S(1)} %dynamic-slice_bitcast_fusion.1), channel_id=1, source_target_pairs={{0,1},{1,2},{2,3},{3,4},{4,5},{5,6},{6,7},{7,0},{8,9},{9,10},{10,1... | collective-permute-start | bytes 860168 | tf_op jit(solution)/shard_map/ppermute | solution.py:204
  165.6 15.4 %collective-permute-start.1 = (bf16[80,1792]{1,0:T(8,128)(2,1)S(1)}, bf16[80,1792]{1,0:T(8,128)(2,1)S(1)}, u32[]{:S(2)}, u32[]{:S(2)}) collective-permute-start(bf16[80,1792]{1,0:T(8,128)(2,1)S(1)} %dynamic-slice_bitcast_fusion.2), channel_id=1, source_target_pairs={{0,7},{1,0},{2,1},{3,2},{4,3},{5,4},{6,5},{7,6},{8,15},{9,8},{10,9... | collective-permute-start | bytes 860168 | tf_op jit(solution)/shard_map/ppermute | solution.py:204
  176.8 15.3 %collective-permute-start.60 = (bf16[80,1792]{1,0:T(8,128)(2,1)S(1)}, bf16[80,1792]{1,0:T(8,128)(2,1)S(1)}, u32[]{:S(2)}, u32[]{:S(2)}) collective-permute-start(bf16[80,1792]{1,0:T(8,128)(2,1)S(1)} %fusion.13), channel_id=1, source_target_pairs={{0,1},{1,2},{2,3},{3,4},{4,5},{5,6},{6,7},{7,0},{8,9},{9,10},{10,1... | collective-permute-start | bytes 860168 | tf_op jit(solution)/shard_map/ppermute | solution.py:204
  176.8 15.4 %collective-permute-start.61 = (bf16[80,1792]{1,0:T(8,128)(2,1)S(1)}, bf16[80,1792]{1,0:T(8,128)(2,1)S(1)}, u32[]{:S(2)}, u32[]{:S(2)}) collective-permute-start(bf16[80,1792]{1,0:T(8,128)(2,1)S(1)} %fusion.12), channel_id=1, source_target_pairs={{0,7},{1,0},{2,1},{3,2},{4,3},{5,4},{6,5},{7,6},{8,15},{9,8},{10,9... | collective-permute-start | bytes 860168 | tf_op jit(solution)/shard_map/ppermute | solution.py:204
  195.6 15.7 %collective-permute-start.64 = (bf16[80,1792]{1,0:T(8,128)(2,1)S(1)}, bf16[80,1792]{1,0:T(8,128)(2,1)S(1)}, u32[]{:S(2)}, u32[]{:S(2)}) collective-permute-start(bf16[80,1792]{1,0:T(8,128)(2,1)S(1)} %fusion.11), channel_id=1, source_target_pairs={{0,1},{1,2},{2,3},{3,4},{4,5},{5,6},{6,7},{7,0},{8,9},{9,10},{10,1... | collective-permute-start | bytes 860168 | tf_op jit(solution)/shard_map/ppermute | solution.py:204
  195.6 15.8 %collective-permute-start.65 = (bf16[80,1792]{1,0:T(8,128)(2,1)S(1)}, bf16[80,1792]{1,0:T(8,128)(2,1)S(1)}, u32[]{:S(2)}, u32[]{:S(2)}) collective-permute-start(bf16[80,1792]{1,0:T(8,128)(2,1)S(1)} %fusion.10), channel_id=1, source_target_pairs={{0,7},{1,0},{2,1},{3,2},{4,3},{5,4},{6,5},{7,6},{8,15},{9,8},{10,9... | collective-permute-start | bytes 860168 | tf_op jit(solution)/shard_map/ppermute | solution.py:204
  215.2 14.5 %collective-permute-start.68 = (bf16[80,1792]{1,0:T(8,128)(2,1)S(1)}, bf16[80,1792]{1,0:T(8,128)(2,1)S(1)}, u32[]{:S(2)}, u32[]{:S(2)}) collective-permute-start(bf16[80,1792]{1,0:T(8,128)(2,1)S(1)} %fusion.9), channel_id=1, source_target_pairs={{0,1},{1,2},{2,3},{3,4},{4,5},{5,6},{6,7},{7,0},{8,9},{9,10},{10,1... | collective-permute-start | bytes 860168 | tf_op jit(solution)/shard_map/ppermute | solution.py:204
  215.2 14.6 %collective-permute-start.69 = (bf16[80,1792]{1,0:T(8,128)(2,1)S(1)}, bf16[80,1792]{1,0:T(8,128)(2,1)S(1)}, u32[]{:S(2)}, u32[]{:S(2)}) collective-permute-start(bf16[80,1792]{1,0:T(8,128)(2,1)S(1)} %fusion.8), channel_id=1, source_target_pairs={{0,7},{1,0},{2,1},{3,2},{4,3},{5,4},{6,5},{7,6},{8,15},{9,8},{10,9... | collective-permute-start | bytes 860168 | tf_op jit(solution)/shard_map/ppermute | solution.py:204
  233.2 14.6 %collective-permute-start.72 = (bf16[80,1792]{1,0:T(8,128)(2,1)S(1)}, bf16[80,1792]{1,0:T(8,128)(2,1)S(1)}, u32[]{:S(2)}, u32[]{:S(2)}) collective-permute-start(bf16[80,1792]{1,0:T(8,128)(2,1)S(1)} %fusion.7), channel_id=1, source_target_pairs={{0,1},{1,2},{2,3},{3,4},{4,5},{5,6},{6,7},{7,0},{8,9},{9,10},{10,1... | collective-permute-start | bytes 860168 | tf_op jit(solution)/shard_map/ppermute | solution.py:204
  234.1 13.8 %collective-permute-start.73 = (bf16[80,1792]{1,0:T(8,128)(2,1)S(1)}, bf16[80,1792]{1,0:T(8,128)(2,1)S(1)}, u32[]{:S(2)}, u32[]{:S(2)}) collective-permute-start(bf16[80,1792]{1,0:T(8,128)(2,1)S(1)} %fusion.6), channel_id=1, source_target_pairs={{0,7},{1,0},{2,1},{3,2},{4,3},{5,4},{6,5},{7,6},{8,15},{9,8},{10,9... | collective-permute-start | bytes 860168 | tf_op jit(solution)/shard_map/ppermute | solution.py:204
  251.7 14.6 %collective-permute-start.76 = (bf16[80,1792]{1,0:T(8,128)(2,1)S(1)}, bf16[80,1792]{1,0:T(8,128)(2,1)S(1)}, u32[]{:S(2)}, u32[]{:S(2)}) collective-permute-start(bf16[80,1792]{1,0:T(8,128)(2,1)S(1)} %fusion.5), channel_id=1, source_target_pairs={{0,1},{1,2},{2,3},{3,4},{4,5},{5,6},{6,7},{7,0},{8,9},{9,10},{10,1... | collective-permute-start | bytes 860168 | tf_op jit(solution)/shard_map/ppermute | solution.py:204
  252.7 13.7 %collective-permute-start.77 = (bf16[80,1792]{1,0:T(8,128)(2,1)S(1)}, bf16[80,1792]{1,0:T(8,128)(2,1)S(1)}, u32[]{:S(2)}, u32[]{:S(2)}) collective-permute-start(bf16[80,1792]{1,0:T(8,128)(2,1)S(1)} %fusion.4), channel_id=1, source_target_pairs={{0,7},{1,0},{2,1},{3,2},{4,3},{5,4},{6,5},{7,6},{8,15},{9,8},{10,9... | collective-permute-start | bytes 860168 | tf_op jit(solution)/shard_map/ppermute | solution.py:204
  270.3 14.5 %collective-permute-start.80 = (bf16[80,1792]{1,0:T(8,128)(2,1)S(1)}, bf16[80,1792]{1,0:T(8,128)(2,1)S(1)}, u32[]{:S(2)}, u32[]{:S(2)}) collective-permute-start(bf16[80,1792]{1,0:T(8,128)(2,1)S(1)} %fusion.3), channel_id=1, source_target_pairs={{0,1},{1,2},{2,3},{3,4},{4,5},{5,6},{6,7},{7,0},{8,9},{9,10},{10,1... | collective-permute-start | bytes 860168 | tf_op jit(solution)/shard_map/ppermute | solution.py:204
  298.1 13.9 %collective-permute-start.28 = (bf16[80,1792]{1,0:T(8,128)(2,1)S(1)}, bf16[80,1792]{1,0:T(8,128)(2,1)S(1)}, u32[]{:S(2)}, u32[]{:S(2)}) collective-permute-start(bf16[80,1792]{1,0:T(8,128)(2,1)S(1)} %fusion.15.gg), channel_id=1, source_target_pairs={{0,1},{1,2},{2,3},{3,4},{4,5},{5,6},{6,7},{7,0},{8,9},{9,10},{10,1... | collective-permute-start | bytes 860168 | tf_op jit(solution)/shard_map/ppermute | solution.py:216
  299.9 15.5 %collective-permute-start.29 = (bf16[80,1792]{1,0:T(8,128)(2,1)S(1)}, bf16[80,1792]{1,0:T(8,128)(2,1)S(1)}, u32[]{:S(2)}, u32[]{:S(2)}) collective-permute-start(bf16[80,1792]{1,0:T(8,128)(2,1)S(1)} %fusion.14.gu), channel_id=1, source_target_pairs={{0,7},{1,0},{2,1},{3,2},{4,3},{5,4},{6,5},{7,6},{8,15},{9,8},{10,9... | collective-permute-start | bytes 860168 | tf_op jit(solution)/shard_map/ppermute | solution.py:216
  302.9 15.9 %collective-permute-start.91 = (bf16[112,640]{1,0:T(8,128)(2,1)S(1)}, bf16[112,640]{1,0:T(8,128)(2,1)S(1)}, u32[]{:S(2)}, u32[]{:S(2)}) collective-permute-start(bf16[112,640]{1,0:T(8,128)(2,1)S(1)} %collective-permute-done.87.gd1), channel_id=1, source_target_pairs={{0,7},{1,0},{2,1},{3,2},{4,3},{5,4},{6,5},{7,6},{8,15},{9,8},{10,9... | collective-permute-start | bytes 430088 | tf_op jit(solution)/shard_map/ppermute | solution.py:216
  305.8 13.7 %collective-permute-start.88 = (bf16[80,1792]{1,0:T(8,128)(2,1)S(1)}, bf16[80,1792]{1,0:T(8,128)(2,1)S(1)}, u32[]{:S(2)}, u32[]{:S(2)}) collective-permute-start(bf16[80,1792]{1,0:T(8,128)(2,1)S(1)} %collective-permute-done.84.gg), channel_id=1, source_target_pairs={{0,1},{1,2},{2,3},{3,4},{4,5},{5,6},{6,7},{7,0},{8,9},{9,10},{10,1... | collective-permute-start | bytes 860168 | tf_op jit(solution)/shard_map/ppermute | solution.py:216
  312.0 16.8 %collective-permute-start.89 = (bf16[80,1792]{1,0:T(8,128)(2,1)S(1)}, bf16[80,1792]{1,0:T(8,128)(2,1)S(1)}, u32[]{:S(2)}, u32[]{:S(2)}) collective-permute-start(bf16[80,1792]{1,0:T(8,128)(2,1)S(1)} %collective-permute-done.85.gu), channel_id=1, source_target_pairs={{0,7},{1,0},{2,1},{3,2},{4,3},{5,4},{6,5},{7,6},{8,15},{9,8},{10,9... | collective-permute-start | bytes 860168 | tf_op jit(solution)/shard_map/ppermute | solution.py:216
  315.5 16.8 %collective-permute-start.35 = (bf16[112,640]{1,0:T(8,128)(2,1)S(1)}, bf16[112,640]{1,0:T(8,128)(2,1)S(1)}, u32[]{:S(2)}, u32[]{:S(2)}) collective-permute-start(bf16[112,640]{1,0:T(8,128)(2,1)S(1)} %collective-permute-done.31.gd1), channel_id=1, source_target_pairs={{0,7},{1,0},{2,1},{3,2},{4,3},{5,4},{6,5},{7,6},{8,15},{9,8},{10,9... | collective-permute-start | bytes 430088 | tf_op jit(solution)/shard_map/ppermute | solution.py:216
  318.8 13.6 %collective-permute-start.32 = (bf16[80,1792]{1,0:T(8,128)(2,1)S(1)}, bf16[80,1792]{1,0:T(8,128)(2,1)S(1)}, u32[]{:S(2)}, u32[]{:S(2)}) collective-permute-start(bf16[80,1792]{1,0:T(8,128)(2,1)S(1)} %collective-permute-done.28.gg), channel_id=1, source_target_pairs={{0,1},{1,2},{2,3},{3,4},{4,5},{5,6},{6,7},{7,0},{8,9},{9,10},{10,1... | collective-permute-start | bytes 860168 | tf_op jit(solution)/shard_map/ppermute | solution.py:216
  319.5 16.2 %collective-permute-start.33 = (bf16[80,1792]{1,0:T(8,128)(2,1)S(1)}, bf16[80,1792]{1,0:T(8,128)(2,1)S(1)}, u32[]{:S(2)}, u32[]{:S(2)}) collective-permute-start(bf16[80,1792]{1,0:T(8,128)(2,1)S(1)} %collective-permute-done.29.gu), channel_id=1, source_target_pairs={{0,7},{1,0},{2,1},{3,2},{4,3},{5,4},{6,5},{7,6},{8,15},{9,8},{10,9... | collective-permute-start | bytes 860168 | tf_op jit(solution)/shard_map/ppermute | solution.py:216
  329.0 16.1 %collective-permute-start.95 = (bf16[112,640]{1,0:T(8,128)(2,1)S(1)}, bf16[112,640]{1,0:T(8,128)(2,1)S(1)}, u32[]{:S(2)}, u32[]{:S(2)}) collective-permute-start(bf16[112,640]{1,0:T(8,128)(2,1)S(1)} %copy-done.67), channel_id=1, source_target_pairs={{0,7},{1,0},{2,1},{3,2},{4,3},{5,4},{6,5},{7,6},{8,15},{9,8},{10,9... | collective-permute-start | bytes 430088 | tf_op jit(solution)/shard_map/ppermute | solution.py:216
  332.4 22.2 %collective-permute-start.93 = (bf16[80,1792]{1,0:T(8,128)(2,1)S(1)}, bf16[80,1792]{1,0:T(8,128)(2,1)S(1)}, u32[]{:S(2)}, u32[]{:S(2)}) collective-permute-start(bf16[80,1792]{1,0:T(8,128)(2,1)S(1)} %collective-permute-done.89.gu), channel_id=1, source_target_pairs={{0,7},{1,0},{2,1},{3,2},{4,3},{5,4},{6,5},{7,6},{8,15},{9,8},{10,9... | collective-permute-start | bytes 860168 | tf_op jit(solution)/shard_map/ppermute | solution.py:216
  335.6 19.2 %collective-permute-start.38 = (bf16[112,640]{1,0:T(8,128)(2,1)S(1)}, bf16[112,640]{1,0:T(8,128)(2,1)S(1)}, u32[]{:S(2)}, u32[]{:S(2)}) collective-permute-start(bf16[112,640]{1,0:T(8,128)(2,1)S(1)} %collective-permute-done.34.gd0), channel_id=1, source_target_pairs={{0,1},{1,2},{2,3},{3,4},{4,5},{5,6},{6,7},{7,0},{8,9},{9,10},{10,1... | collective-permute-start | bytes 430088 | tf_op jit(solution)/shard_map/ppermute | solution.py:216
  341.8 16.2 %collective-permute-start.39 = (bf16[112,640]{1,0:T(8,128)(2,1)S(1)}, bf16[112,640]{1,0:T(8,128)(2,1)S(1)}, u32[]{:S(2)}, u32[]{:S(2)}) collective-permute-start(bf16[112,640]{1,0:T(8,128)(2,1)S(1)} %collective-permute-done.35.gd1), channel_id=1, source_target_pairs={{0,7},{1,0},{2,1},{3,2},{4,3},{5,4},{6,5},{7,6},{8,15},{9,8},{10,9... | collective-permute-start | bytes 430088 | tf_op jit(solution)/shard_map/ppermute | solution.py:216
  345.2 16.2 %collective-permute-start.37 = (bf16[80,1792]{1,0:T(8,128)(2,1)S(1)}, bf16[80,1792]{1,0:T(8,128)(2,1)S(1)}, u32[]{:S(2)}, u32[]{:S(2)}) collective-permute-start(bf16[80,1792]{1,0:T(8,128)(2,1)S(1)} %collective-permute-done.33.gu), channel_id=1, source_target_pairs={{0,7},{1,0},{2,1},{3,2},{4,3},{5,4},{6,5},{7,6},{8,15},{9,8},{10,9... | collective-permute-start | bytes 860168 | tf_op jit(solution)/shard_map/ppermute | solution.py:216
  354.8 16.1 %collective-permute-start.99 = (bf16[112,640]{1,0:T(8,128)(2,1)S(1)}, bf16[112,640]{1,0:T(8,128)(2,1)S(1)}, u32[]{:S(2)}, u32[]{:S(2)}) collective-permute-start(bf16[112,640]{1,0:T(8,128)(2,1)S(1)} %collective-permute-done.95.gd1), channel_id=1, source_target_pairs={{0,7},{1,0},{2,1},{3,2},{4,3},{5,4},{6,5},{7,6},{8,15},{9,8},{10,9... | collective-permute-start | bytes 430088 | tf_op jit(solution)/shard_map/ppermute | solution.py:216
  358.2 22.2 %collective-permute-start.97 = (bf16[80,1792]{1,0:T(8,128)(2,1)S(1)}, bf16[80,1792]{1,0:T(8,128)(2,1)S(1)}, u32[]{:S(2)}, u32[]{:S(2)}) collective-permute-start(bf16[80,1792]{1,0:T(8,128)(2,1)S(1)} %collective-permute-done.93.gu), channel_id=1, source_target_pairs={{0,7},{1,0},{2,1},{3,2},{4,3},{5,4},{6,5},{7,6},{8,15},{9,8},{10,9... | collective-permute-start | bytes 860168 | tf_op jit(solution)/shard_map/ppermute | solution.py:216
  361.4 19.2 %collective-permute-start.42 = (bf16[112,640]{1,0:T(8,128)(2,1)S(1)}, bf16[112,640]{1,0:T(8,128)(2,1)S(1)}, u32[]{:S(2)}, u32[]{:S(2)}) collective-permute-start(bf16[112,640]{1,0:T(8,128)(2,1)S(1)} %collective-permute-done.38.gd0), channel_id=1, source_target_pairs={{0,1},{1,2},{2,3},{3,4},{4,5},{5,6},{6,7},{7,0},{8,9},{9,10},{10,1... | collective-permute-start | bytes 430088 | tf_op jit(solution)/shard_map/ppermute | solution.py:216
  367.6 16.3 %collective-permute-start.43 = (bf16[112,640]{1,0:T(8,128)(2,1)S(1)}, bf16[112,640]{1,0:T(8,128)(2,1)S(1)}, u32[]{:S(2)}, u32[]{:S(2)}) collective-permute-start(bf16[112,640]{1,0:T(8,128)(2,1)S(1)} %collective-permute-done.39.gd1), channel_id=1, source_target_pairs={{0,7},{1,0},{2,1},{3,2},{4,3},{5,4},{6,5},{7,6},{8,15},{9,8},{10,9... | collective-permute-start | bytes 430088 | tf_op jit(solution)/shard_map/ppermute | solution.py:216
  371.1 16.2 %collective-permute-start.41 = (bf16[80,1792]{1,0:T(8,128)(2,1)S(1)}, bf16[80,1792]{1,0:T(8,128)(2,1)S(1)}, u32[]{:S(2)}, u32[]{:S(2)}) collective-permute-start(bf16[80,1792]{1,0:T(8,128)(2,1)S(1)} %collective-permute-done.37.gu), channel_id=1, source_target_pairs={{0,7},{1,0},{2,1},{3,2},{4,3},{5,4},{6,5},{7,6},{8,15},{9,8},{10,9... | collective-permute-start | bytes 860168 | tf_op jit(solution)/shard_map/ppermute | solution.py:216
  380.6 16.3 %collective-permute-start.103 = (bf16[112,640]{1,0:T(8,128)(2,1)S(1)}, bf16[112,640]{1,0:T(8,128)(2,1)S(1)}, u32[]{:S(2)}, u32[]{:S(2)}) collective-permute-start(bf16[112,640]{1,0:T(8,128)(2,1)S(1)} %collective-permute-done.99.gd1), channel_id=1, source_target_pairs={{0,7},{1,0},{2,1},{3,2},{4,3},{5,4},{6,5},{7,6},{8,15},{9,8},{10,9... | collective-permute-start | bytes 430088 | tf_op jit(solution)/shard_map/ppermute | solution.py:216
  384.0 22.4 %collective-permute-start.101 = (bf16[80,1792]{1,0:T(8,128)(2,1)S(1)}, bf16[80,1792]{1,0:T(8,128)(2,1)S(1)}, u32[]{:S(2)}, u32[]{:S(2)}) collective-permute-start(bf16[80,1792]{1,0:T(8,128)(2,1)S(1)} %collective-permute-done.97.gu), channel_id=1, source_target_pairs={{0,7},{1,0},{2,1},{3,2},{4,3},{5,4},{6,5},{7,6},{8,15},{9,8},{10,9... | collective-permute-start | bytes 860168 | tf_op jit(solution)/shard_map/ppermute | solution.py:216
  387.3 19.3 %collective-permute-start.46 = (bf16[112,640]{1,0:T(8,128)(2,1)S(1)}, bf16[112,640]{1,0:T(8,128)(2,1)S(1)}, u32[]{:S(2)}, u32[]{:S(2)}) collective-permute-start(bf16[112,640]{1,0:T(8,128)(2,1)S(1)} %collective-permute-done.42.gd0), channel_id=1, source_target_pairs={{0,1},{1,2},{2,3},{3,4},{4,5},{5,6},{6,7},{7,0},{8,9},{9,10},{10,1... | collective-permute-start | bytes 430088 | tf_op jit(solution)/shard_map/ppermute | solution.py:216
  393.7 16.2 %collective-permute-start.47 = (bf16[112,640]{1,0:T(8,128)(2,1)S(1)}, bf16[112,640]{1,0:T(8,128)(2,1)S(1)}, u32[]{:S(2)}, u32[]{:S(2)}) collective-permute-start(bf16[112,640]{1,0:T(8,128)(2,1)S(1)} %collective-permute-done.43.gd1), channel_id=1, source_target_pairs={{0,7},{1,0},{2,1},{3,2},{4,3},{5,4},{6,5},{7,6},{8,15},{9,8},{10,9... | collective-permute-start | bytes 430088 | tf_op jit(solution)/shard_map/ppermute | solution.py:216
  397.0 16.2 %collective-permute-start.45 = (bf16[80,1792]{1,0:T(8,128)(2,1)S(1)}, bf16[80,1792]{1,0:T(8,128)(2,1)S(1)}, u32[]{:S(2)}, u32[]{:S(2)}) collective-permute-start(bf16[80,1792]{1,0:T(8,128)(2,1)S(1)} %collective-permute-done.41.gu), channel_id=1, source_target_pairs={{0,7},{1,0},{2,1},{3,2},{4,3},{5,4},{6,5},{7,6},{8,15},{9,8},{10,9... | collective-permute-start | bytes 860168 | tf_op jit(solution)/shard_map/ppermute | solution.py:216
  406.6 16.1 %collective-permute-start.107 = (bf16[112,640]{1,0:T(8,128)(2,1)S(1)}, bf16[112,640]{1,0:T(8,128)(2,1)S(1)}, u32[]{:S(2)}, u32[]{:S(2)}) collective-permute-start(bf16[112,640]{1,0:T(8,128)(2,1)S(1)} %collective-permute-done.103.gd1), channel_id=1, source_target_pairs={{0,7},{1,0},{2,1},{3,2},{4,3},{5,4},{6,5},{7,6},{8,15},{9,8},{10,9... | collective-permute-start | bytes 430088 | tf_op jit(solution)/shard_map/ppermute | solution.py:216
  410.0 22.2 %collective-permute-start.105 = (bf16[80,1792]{1,0:T(8,128)(2,1)S(1)}, bf16[80,1792]{1,0:T(8,128)(2,1)S(1)}, u32[]{:S(2)}, u32[]{:S(2)}) collective-permute-start(bf16[80,1792]{1,0:T(8,128)(2,1)S(1)} %collective-permute-done.101.gu), channel_id=1, source_target_pairs={{0,7},{1,0},{2,1},{3,2},{4,3},{5,4},{6,5},{7,6},{8,15},{9,8},{10,9... | collective-permute-start | bytes 860168 | tf_op jit(solution)/shard_map/ppermute | solution.py:216
  413.2 19.2 %collective-permute-start.50 = (bf16[112,640]{1,0:T(8,128)(2,1)S(1)}, bf16[112,640]{1,0:T(8,128)(2,1)S(1)}, u32[]{:S(2)}, u32[]{:S(2)}) collective-permute-start(bf16[112,640]{1,0:T(8,128)(2,1)S(1)} %collective-permute-done.46.gd0), channel_id=1, source_target_pairs={{0,1},{1,2},{2,3},{3,4},{4,5},{5,6},{6,7},{7,0},{8,9},{9,10},{10,1... | collective-permute-start | bytes 430088 | tf_op jit(solution)/shard_map/ppermute | solution.py:216
  419.5 16.2 %collective-permute-start.51 = (bf16[112,640]{1,0:T(8,128)(2,1)S(1)}, bf16[112,640]{1,0:T(8,128)(2,1)S(1)}, u32[]{:S(2)}, u32[]{:S(2)}) collective-permute-start(bf16[112,640]{1,0:T(8,128)(2,1)S(1)} %collective-permute-done.47.gd1), channel_id=1, source_target_pairs={{0,7},{1,0},{2,1},{3,2},{4,3},{5,4},{6,5},{7,6},{8,15},{9,8},{10,9... | collective-permute-start | bytes 430088 | tf_op jit(solution)/shard_map/ppermute | solution.py:216
  422.9 16.2 %collective-permute-start.49 = (bf16[80,1792]{1,0:T(8,128)(2,1)S(1)}, bf16[80,1792]{1,0:T(8,128)(2,1)S(1)}, u32[]{:S(2)}, u32[]{:S(2)}) collective-permute-start(bf16[80,1792]{1,0:T(8,128)(2,1)S(1)} %collective-permute-done.45.gu), channel_id=1, source_target_pairs={{0,7},{1,0},{2,1},{3,2},{4,3},{5,4},{6,5},{7,6},{8,15},{9,8},{10,9... | collective-permute-start | bytes 860168 | tf_op jit(solution)/shard_map/ppermute | solution.py:216
  432.4 16.1 %collective-permute-start.111 = (bf16[112,640]{1,0:T(8,128)(2,1)S(1)}, bf16[112,640]{1,0:T(8,128)(2,1)S(1)}, u32[]{:S(2)}, u32[]{:S(2)}) collective-permute-start(bf16[112,640]{1,0:T(8,128)(2,1)S(1)} %collective-permute-done.107.gd1), channel_id=1, source_target_pairs={{0,7},{1,0},{2,1},{3,2},{4,3},{5,4},{6,5},{7,6},{8,15},{9,8},{10,9... | collective-permute-start | bytes 430088 | tf_op jit(solution)/shard_map/ppermute | solution.py:216
  435.8 22.4 %collective-permute-start.109 = (bf16[80,1792]{1,0:T(8,128)(2,1)S(1)}, bf16[80,1792]{1,0:T(8,128)(2,1)S(1)}, u32[]{:S(2)}, u32[]{:S(2)}) collective-permute-start(bf16[80,1792]{1,0:T(8,128)(2,1)S(1)} %collective-permute-done.105.gu), channel_id=1, source_target_pairs={{0,7},{1,0},{2,1},{3,2},{4,3},{5,4},{6,5},{7,6},{8,15},{9,8},{10,9... | collective-permute-start | bytes 860168 | tf_op jit(solution)/shard_map/ppermute | solution.py:216
  439.0 19.3 %collective-permute-start.54 = (bf16[112,640]{1,0:T(8,128)(2,1)S(1)}, bf16[112,640]{1,0:T(8,128)(2,1)S(1)}, u32[]{:S(2)}, u32[]{:S(2)}) collective-permute-start(bf16[112,640]{1,0:T(8,128)(2,1)S(1)} %collective-permute-done.50.gd0), channel_id=1, source_target_pairs={{0,1},{1,2},{2,3},{3,4},{4,5},{5,6},{6,7},{7,0},{8,9},{9,10},{10,1... | collective-permute-start | bytes 430088 | tf_op jit(solution)/shard_map/ppermute | solution.py:216
  (141 other events, 1740.0 us)
